TPU v7x, 32 devices: a whole 2x2x4 slice. The times are simulated.
32 devices in a mesh: dp: 8 (over z, y), mp: 4 (over x, core).
Axes of the slice: x: 2, y: 2, z: 4, core: 2. Of those that a mesh axis runs over, the one named last changes fastest.
Arguments:
- gradients: bfloat16 [4, 16, 1024, 1024], P(None, 'mp', 'dp'), as said below
- statistics: float32 [4, 32, 1024, 1024], P('mp', 'dp'), as said below
- accumulator: float32 [4, 16, 1024, 1024], P(None, 'mp', 'dp'), may hold values from 0.25 to 4
Outputs:
- update: float32 [4, 16, 1024, 1024], P(None, 'mp', 'dp')
- statistics_new: float32 [4, 32, 1024, 1024], P('mp', 'dp')
- accumulator_new: float32 [4, 16, 1024, 1024], P(None, 'mp', 'dp')
Inputs may be any that keep to these rules, and one draw needn't show every extreme that they name: `gradients`: Real-valued gradient blocks. `statistics`: each 1024 x 1024 statistic is symmetric positive definite.
All inputs are finite; a program needn't handle non-finite values.
Results may differ from a plain program's by a relative error of at most 0.005.
The roundings to bfloat16 on the way count: a program that leaves them out, or rounds other values in their place, can miss the bound.
Values may be sent and summed in bfloat16 or wider, within the bound.
No kernel may reach another device: no remote copies, remote signals or barrier semaphores. Data moves between devices by JAX's collectives and lax.ppermute only.
A program may use at most 192 MiB of HBM per device.

v0:
```python
import jax
import jax.numpy as jnp
from jax import lax
from jax.sharding import PartitionSpec as P

ITERS = 3


def partner_2(value, axis, distance):
    return lax.ppermute(value, axis, [(i, i ^ 1 << distance) for i in range(lax.axis_size(axis))])


def batch_dot(left, right):
    return jnp.einsum("kij,kjl->kil", left, right, preferred_element_type=jnp.float32)


def inverse_roots(statistic):
    block_width = statistic.shape[-1]
    identity = jnp.eye(block_width, dtype=jnp.float32)
    frob_norms = jnp.sqrt(jnp.sum(statistic * statistic, axis=(1, 2)) + 1e-06)
    newton_scale = (2.5 / frob_norms)[:, None, None]
    matrix = newton_scale * statistic
    root_iter = jnp.sqrt(jnp.sqrt(newton_scale)) * identity
    for iteration in range(ITERS):
        factor = (1.25 * identity - 0.25 * matrix).astype(jnp.bfloat16)
        root_iter = batch_dot(root_iter.astype(jnp.bfloat16), factor)
        if iteration + 1 < ITERS:
            square = batch_dot(factor, factor).astype(jnp.bfloat16)
            fourth = batch_dot(square, square).astype(jnp.bfloat16)
            matrix = batch_dot(fourth, matrix.astype(jnp.bfloat16))
    return root_iter


def on_device(gradients, statistics, accumulator):
    owners = lax.axis_size("dp")
    own_index = lax.axis_index("dp")
    row_blocks, col_blocks, dev_rows, block_width = gradients.shape
    blocks = row_blocks * col_blocks
    owned_factors = statistics.shape[1]
    split_pairs = owned_factors == 1
    half_rows = dev_rows // 2
    parity = own_index % 2
    left_side = parity == 0
    by_block = gradients.reshape(blocks, dev_rows, block_width)
    grads_wide = gradients.astype(jnp.float32)
    grad_total = lax.psum(jnp.sum(grads_wide * grads_wide), ("dp", "mp"))
    entries = blocks * dev_rows * block_width * owners * lax.axis_size("mp")
    clip_factor = jnp.minimum(1.0, jnp.sqrt(entries / (grad_total + 1e-06)))
    scaled = clip_factor * grads_wide
    accumulated = accumulator + scaled * scaled
    graft_step = scaled / jnp.sqrt(accumulated)
    graft_squares = jnp.sum(graft_step * graft_step)
    row_parts = 2 if split_pairs else 1
    row_units = by_block.reshape(blocks * row_parts, dev_rows // row_parts, block_width)
    received = lax.all_to_all(row_units, "dp", split_axis=0, concat_axis=1, tiled=True)
    if split_pairs:
        partner_part = partner_2(received, "dp", 0)
        own_part = received.reshape(owners, 1, half_rows, block_width)
        partner_part = partner_part.reshape(owners, 1, half_rows, block_width)
        ordered = jnp.where(
            left_side,
            jnp.concatenate([own_part, partner_part], 1),
            jnp.concatenate([partner_part, own_part], 1),
        )
        whole_blocks = ordered.reshape(1, owners * dev_rows, block_width)
    else:
        whole_blocks = received
    transposed = jnp.swapaxes(whole_blocks, 1, 2)
    if split_pairs:
        factor_inputs = jnp.where(left_side, whole_blocks, transposed)
    else:
        factor_inputs = jnp.stack([whole_blocks, transposed], 1).reshape(
            owned_factors, block_width, block_width
        )
    gram_matrix = jnp.einsum(
        "kij,klj->kil", factor_inputs, factor_inputs, preferred_element_type=jnp.float32
    )
    statistics_new = (
        0.9 * statistics[0] + 0.1 / block_width * clip_factor * clip_factor * gram_matrix
    )
    root_values = inverse_roots(statistics_new).astype(jnp.bfloat16)
    if split_pairs:
        partner = partner_2(root_values, "dp", 0)
        left_root = jnp.where(left_side, root_values, partner)[0]
        right_root = jnp.where(left_side, partner, root_values)[0]
        left_rows = lax.dynamic_slice_in_dim(
            left_root.reshape(owners, 2, half_rows, block_width), parity, 1, 1
        )
        left_rows = left_rows.reshape(owners * half_rows, block_width)
        left_applied = jnp.dot(
            left_rows, whole_blocks[0], preferred_element_type=jnp.float32
        ).astype(jnp.bfloat16)
        product = jnp.dot(left_applied, right_root, preferred_element_type=jnp.float32)
        pieces = product.reshape(1, owners, half_rows, block_width)
    else:
        root_pairs = root_values.reshape(-1, 2, block_width, block_width)
        left_applied = batch_dot(root_pairs[:, 0], whole_blocks).astype(jnp.bfloat16)
        product = batch_dot(left_applied, root_pairs[:, 1])
        pieces = product.reshape(-1, owners, dev_rows, block_width)
    returned = lax.all_to_all(
        pieces.astype(jnp.bfloat16), "dp", split_axis=1, concat_axis=0, tiled=True
    ).astype(pieces.dtype)
    returned = returned.reshape(row_blocks, col_blocks, dev_rows, block_width)
    graft_total, update_total = lax.psum(
        (graft_squares, jnp.sum(returned * returned)), ("dp", "mp")
    )
    graft_ratio = jnp.sqrt(graft_total / (update_total + 1e-06))
    return (graft_ratio * returned, statistics_new[None], accumulated)


def solution(mesh):
    return jax.shard_map(
        on_device,
        mesh=mesh,
        in_specs=(P(None, "mp", "dp", None), P("mp", "dp", None, None), P(None, "mp", "dp", None)),
        out_specs=(P(None, "mp", "dp", None), P("mp", "dp", None, None), P(None, "mp", "dp", None)),
        check_vma=False,
    )
```

profile of v0, /device:TPU:12, one launch (start us, length us, event | category | flops | bytes accessed | tf_op | source)
XLA Modules:
  0.0 485.6 jit_solution(2648131232850951314)
XLA Ops:
  0.6 6.2 %all-to-all-start = ((bf16[16,128,1024]{2,1,0:T(8,128)(2,1)}), bf16[16,128,1024]{2,1,0:T(8,128)(2,1)}, u32[]{:S(2)}, u32[]{:S(2)}) async-start(bf16[16,128,1024]{2,1,0:T(8,128)(2,1)} %bitcast.47), calls=%async_computation | async-start | bytes 8388608 | tf_op jit(solution)/shard_map/all_to_all | solution.py:55
  6.9 5.0 %fusion.5 = f32[]{:T(128)} fusion(bf16[4,4,128,1024]{3,2,1,0:T(8,128)(2,1)} %param.3), kind=kLoop, calls=%fused_computation.16 | loop fusion | flops 6291455 | bytes 4194308 | tf_op jit(solution)/shard_map/reduce_sum | solution.py:46
  11.8 107.4 %psum.21 = f32[]{:T(128)} all-reduce(f32[]{:T(128)} %fusion.5), channel_id=1, replica_groups=mesh['dp'=8,'mp'=4] {'dp','mp'}, use_global_device_ids=true, to_apply=%region_1.0 | all-reduce | flops 1 | bytes 8 | tf_op jit(solution)/shard_map/psum | solution.py:46
  120.0 2.5 fusion.33
  122.4 2.4 fusion.34
  124.9 6.7 %copy.10 = bf16[8,2,128,1024]{2,0,3,1:T(8,128)(2,1)} copy(bf16[8,2,128,1024]{3,2,1,0:T(8,128)(2,1)} %bitcast.2) | data formatting | bytes 8388608 | tf_op jit(solution)/shard_map/all_to_all | solution.py:55
  131.6 7.3 %all_to_all.23 = bf16[2,1024,1024]{1,2,0:T(8,128)(2,1)} reshape(bf16[2,8,128,1024]{2,1,3,0:T(8,128)(2,1)} %bitcast.48) | data formatting | bytes 8388608 | tf_op jit(solution)/shard_map/all_to_all | solution.py:55
  139.0 5.0 %copy.11 = bf16[2,8,128,1024]{3,2,1,0:T(8,128)(2,1)} copy(bf16[2,8,128,1024]{3,2,0,1:T(8,128)(2,1)} %bitcast.4) | data formatting | bytes 8388608 | tf_op jit(solution)/shard_map/all_to_all | solution.py:55
  143.9 6.3 %pad_maximum_fusion = bf16[2,2,1024,1024]{3,2,1,0:T(8,128)(2,1)} fusion(bf16[2,1,1024,1024]{3,2,1,0:T(8,128)(2,1)S(1)} %bitcast.49, bf16[2,1,1024,1024]{3,2,1,0:T(8,128)(2,1)} %bitcast.50), kind=kLoop, calls=%fused_computation.20 | loop fusion | flops 4194304 | bytes 16777216 | tf_op jit(solution)/shard_map/stack | solution.py:72
  150.3 22.7 %multiply_reduce_fusion = (f32[4]{0:T(128)S(1)}, f32[4,1024,1024]{2,1,0:T(8,128)}) fusion(bf16[4,1024,1024]{2,1,0:T(8,128)(2,1)} %bitcast.52, f32[]{:T(128)S(6)} %mul.104, f32[1,4,1024,1024]{3,2,1,0:T(8,128)} %param.4), kind=kOutput, calls=%fused_computation.5 | convolution fusion | flops 8610906112 | bytes 41943060 | tf_op jit(solution)/shard_map/kij,klj->kil/dot_general | solution.py:75
  172.9 22.1 %fusion.46 = bf16[4,1024,1024]{2,1,0:T(8,128)(2,1)} fusion(f32[4,1024,1024]{2,1,0:T(8,128)} %get-tuple-element.10, f32[4]{0:T(128)S(1)} %get-tuple-element.8, f32[1024,1024]{1,0:T(8,128)} %fusion.33), kind=kOutput, calls=%fused_computation.50 | convolution fusion | flops 8606711808 | bytes 29360144 | tf_op jit(solution)/shard_map/kij,kjl->kil/dot_general | solution.py:14
  195.0 24.0 %fusion.7 = f32[4,1024,1024]{2,1,0:T(8,128)} fusion(f32[4,1024,1024]{2,1,0:T(8,128)} %get-tuple-element.10, bf16[4,1024,1024]{2,1,0:T(8,128)(2,1)} %fusion.46, f32[4]{0:T(128)S(1)} %get-tuple-element.8), kind=kOutput, calls=%fused_computation.18 | convolution fusion | flops 17192452096 | bytes 41943056 | tf_op jit(solution)/shard_map/kij,kjl->kil/dot_general | solution.py:14
  219.0 21.3 %fusion.42 = bf16[4,1024,1024]{2,1,0:T(8,128)(2,1)} fusion(f32[4,1024,1024]{2,1,0:T(8,128)} %fusion.7, f32[1024,1024]{1,0:T(8,128)} %fusion.33), kind=kOutput, calls=%fused_computation.45 | convolution fusion | flops 8602517504 | bytes 29360128 | tf_op jit(solution)/shard_map/kij,kjl->kil/dot_general | solution.py:14
  240.3 28.1 %subtract_convert_fusion = bf16[4,1024,1024]{2,1,0:T(8,128)(2,1)} fusion(f32[4,1024,1024]{2,1,0:T(8,128)} %fusion.7, bf16[4,1024,1024]{2,1,0:T(8,128)(2,1)} %fusion.42, f32[1024,1024]{1,0:T(8,128)} %fusion.33), kind=kOutput, calls=%fused_computation.1 | convolution fusion | flops 17200840704 | bytes 37748736 | tf_op jit(solution)/shard_map/kij,kjl->kil/dot_general | solution.py:14
  268.4 19.1 %fusion.8 = bf16[4,1024,1024]{2,1,0:T(8,128)(2,1)} fusion(f32[1024,1024]{1,0:T(8,128)} %fusion.34, f32[4]{0:T(128)S(1)} %get-tuple-element.7, f32[4,1024,1024]{2,1,0:T(8,128)} %get-tuple-element.10, f32[4]{0:T(128)S(1)} %get-tuple-element.8, f32[1024,1024]{1,0:T(8,128)} %fusion.33), kind=kOutput, calls=%fused_computation.19 | convolution fusion | flops 8615100416 | bytes 33554464 | tf_op jit(solution)/shard_map/kij,kjl->kil/dot_general | solution.py:14
  287.4 28.1 %fusion.27 = bf16[4,1024,1024]{2,1,0:T(8,128)(2,1)} fusion(bf16[4,1024,1024]{2,1,0:T(8,128)(2,1)} %subtract_convert_fusion, bf16[4,1024,1024]{2,1,0:T(8,128)(2,1)} %fusion.8, f32[4,1024,1024]{2,1,0:T(8,128)} %fusion.7, f32[1024,1024]{1,0:T(8,128)} %fusion.33), kind=kOutput, calls=%fused_computation.35 | convolution fusion | flops 17200840704 | bytes 46137344 | tf_op jit(solution)/shard_map/kij,kjl->kil/dot_general | solution.py:14
  315.5 13.3 %fusion.39 = bf16[2,1024,1024]{2,1,0:T(8,128)(2,1)} fusion(bf16[2,2,1024,1024]{3,2,1,0:T(8,128)(2,1)} %bitcast.55, bf16[2,1024,1024]{1,2,0:T(8,128)(2,1)} %all_to_all.23), kind=kOutput, calls=%fused_computation.44 | convolution fusion | flops 8594128896 | bytes 16777216 | tf_op jit(solution)/shard_map/kij,kjl->kil/dot_general | solution.py:14
  328.8 4.8 copy.13
  333.6 6.5 %all-to-all-start.1 = ((bf16[2,8,128,1024]{3,2,0,1:T(8,128)(2,1)}), bf16[2,8,128,1024]{3,2,0,1:T(8,128)(2,1)}, u32[]{:S(2)}, u32[]{:S(2)}) async-start(bf16[2,8,128,1024]{3,2,0,1:T(8,128)(2,1)} %copy.13), calls=%async_computation.1 | async-start | bytes 8388608 | tf_op jit(solution)/shard_map/all_to_all | solution.py:100
  340.1 8.4 %fusion.4 = (f32[]{:T(128)}, f32[4,4,128,1024]{3,2,1,0:T(8,128)}) fusion(bf16[4,4,128,1024]{3,2,1,0:T(8,128)(2,1)} %param.3, f32[]{:T(128)S(6)} %min_shard_map.3, f32[4,4,128,1024]{3,2,1,0:T(8,128)} %param.5), kind=kLoop, calls=%fused_computation.15 | loop fusion | flops 14680063 | bytes 20971528 | tf_op jit(solution)/shard_map/reduce_sum | solution.py:52
  348.5 80.1 %all-to-all-done.1 = bf16[2,8,128,1024]{3,2,0,1:T(8,128)(2,1)} async-done(((bf16[2,8,128,1024]{3,2,0,1:T(8,128)(2,1)}), bf16[2,8,128,1024]{3,2,0,1:T(8,128)(2,1)}, u32[]{:S(2)}, u32[]{:S(2)}) %all-to-all-start.1) | async-done | bytes 4194336 | tf_op jit(solution)/shard_map/all_to_all | solution.py:100
  428.6 5.0 %fusion.6 = f32[]{:T(128)} fusion(bf16[2,8,128,1024]{3,2,0,1:T(8,128)(2,1)} %all-to-all-done.1), kind=kLoop, calls=%fused_computation.17 | loop fusion | flops 6291455 | bytes 4194308 | tf_op jit(solution)/shard_map/reduce_sum | solution.py:105
  433.6 43.9 %all-reduce = (f32[]{:T(128)}, f32[]{:T(128)}) all-reduce(f32[]{:T(128)} %get-tuple-element.5, f32[]{:T(128)} %fusion.6), channel_id=1, replica_groups=mesh['dp'=8,'mp'=4] {'dp','mp'}, use_global_device_ids=true, to_apply=%region_3.0 | all-reduce | flops 2 | bytes 16 | tf_op jit(solution)/shard_map/psum | solution.py:104
  478.8 6.8 %convert_multiply_fusion = f32[2,8,128,1024]{3,2,0,1:T(8,128)} fusion(bf16[2,8,128,1024]{3,2,0,1:T(8,128)(2,1)} %all-to-all-done.1, f32[]{:T(128)S(6)} %sqrt.33), kind=kLoop, calls=%fused_computation.7 | loop fusion | flops 4194304 | bytes 12582916 | tf_op jit(solution)/shard_map/mul | solution.py:108
  (4 shorter events, 0.0 us)
Async XLA Ops:
  0.6 124.3 %all-to-all-start = ((bf16[16,128,1024]{2,1,0:T(8,128)(2,1)}), bf16[16,128,1024]{2,1,0:T(8,128)(2,1)}, u32[]{:S(2)}, u32[]{:S(2)}) async-start(bf16[16,128,1024]{2,1,0:T(8,128)(2,1)} %bitcast.47), calls=%async_computation | async-start | bytes 8388608 | tf_op jit(solution)/shard_map/all_to_all | solution.py:55
  139.0 5.0 %copy-start = (bf16[2,1024,1024]{1,2,0:T(8,128)(2,1)S(1)}, bf16[2,1024,1024]{1,2,0:T(8,128)(2,1)}, u32[]{:S(2)}) copy-start(bf16[2,1024,1024]{1,2,0:T(8,128)(2,1)} %all_to_all.23) | copy-start | bytes 12582916
  333.6 95.0 %all-to-all-start.1 = ((bf16[2,8,128,1024]{3,2,0,1:T(8,128)(2,1)}), bf16[2,8,128,1024]{3,2,0,1:T(8,128)(2,1)}, u32[]{:S(2)}, u32[]{:S(2)}) async-start(bf16[2,8,128,1024]{3,2,0,1:T(8,128)(2,1)} %copy.13), calls=%async_computation.1 | async-start | bytes 8388608 | tf_op jit(solution)/shard_map/all_to_all | solution.py:100
where the time goes:
time: 487 us; the launch traced here: 486 us
  matrix products  179 us (37%)
  blocking collectives  151 us (31%)
  waiting for transfers between devices  80.1 us (16%)
  other arithmetic  36.4 us (7%)
  local copies, waits for them, and re-layouts  23.8 us (5%)
  starting transfers between devices  12.8 us (3%)
    dot_general x7, matrix products, batch_dot(): jnp.einsum('kij,kjl->kil', left, right, preferred_element_type=jnp.float32)  156 us
    psum x1, blocking collectives, on_device(): grad_total = lax.psum(jnp.sum(grads_wide * grads_wide), ('dp', 'mp'))  107 us
    all_to_all x1, waiting for transfers between devices, on_device(): lax.all_to_all(pieces.astype(jnp.bfloat16), 'dp', split_axis=1, concat_ax...  80.1 us
    psum x1, blocking collectives, on_device(): lax.psum((graft_squares, jnp.sum(returned * returned)), ('dp', 'mp'))  43.9 us
    dot_general x1, matrix products, on_device(): jnp.einsum('kij,klj->kil', factor_inputs, factor_inputs, preferred_elemen...  22.7 us
    all_to_all x3, local copies, waits for them, and re-layouts, on_device(): lax.all_to_all(row_units, 'dp', split_axis=0, concat_axis=1, tiled=True)  19 us
  transfers between devices with their start and end apart: 2, of which 1 were waited for; matrix products, arithmetic and copies ran while one was open for 4% of the time, Pallas kernels for 0%

commit v1 on v0

--- a/solution.py
+++ b/solution.py
@@ -1,9 +1,15 @@
+import functools
+
 import jax
 import jax.numpy as jnp
 from jax import lax
+from jax.experimental import pallas as pl
+from jax.experimental.pallas import tpu as pltpu
 from jax.sharding import PartitionSpec as P
 
+
 ITERS = 3
+PANEL = 256
 
 
 def partner_2(value, axis, distance):
@@ -31,7 +37,7 @@
     return root_iter
 
 
-def on_device(gradients, statistics, accumulator):
+def on_device_plain(gradients, statistics, accumulator):
     owners = lax.axis_size("dp")
     own_index = lax.axis_index("dp")
     row_blocks, col_blocks, dev_rows, block_width = gradients.shape
@@ -108,9 +114,214 @@
     return (graft_ratio * returned, statistics_new[None], accumulated)
 
 
+def eye_tile(n):
+    rows = lax.broadcasted_iota(jnp.int32, (n, n), 0)
+    cols = lax.broadcasted_iota(jnp.int32, (n, n), 1)
+    return rows == cols
+
+
+def dot_f32(left, right):
+    return jnp.dot(left, right, preferred_element_type=jnp.float32)
+
+
+def panels(width):
+    return [(start, start + PANEL) for start in range(0, width, PANEL)]
+
+
+def store_symmetric(ref, upper, start, stop):
+    ref[:stop, start:stop] = upper
+    if start:
+        ref[start:stop, :start] = upper[:start].T
+
+
+def block_kernel(block, scale_ref, grad_hbm, stat_hbm, *rest):
+    (stat_out, prod_out, squares_out,
+     grad, grad_t, stat, mats, facs, roots, square, fourth, prod,
+     sem_g, sem_s, sem_o, sem_p) = rest[-16:]
+    width = grad.shape[0]
+    grad_in = pltpu.make_async_copy(grad_hbm, grad, sem_g)
+    grad_in.start()
+    stat_in = [pltpu.make_async_copy(stat_hbm.at[2 * block + s], stat.at[s], sem_s.at[s]) for s in range(2)]
+    for copy in stat_in:
+        copy.start()
+    grad_in.wait()
+    scale = scale_ref[0]
+    grad_t[...] = grad[...].T
+    frob = []
+    stat_done = []
+    for s, (left, right) in enumerate(((grad, grad_t), (grad_t, grad))):
+        stat_in[s].wait()
+        total = jnp.zeros((1, 1), jnp.float32)
+        for start, stop in panels(width):
+            gram = scale * dot_f32(left[:stop, :], right[:, start:stop])
+            upper = 0.9 * stat[s, :stop, start:stop] + gram
+            stat[s, :stop, start:stop] = upper
+            diag = upper[start:]
+            total = total + jnp.sum(diag * diag, keepdims=True)
+            if start:
+                lower = 0.9 * stat[s, start:stop, :start] + gram[:start].T
+                stat[s, start:stop, :start] = lower
+                total = total + jnp.sum(upper[:start] * upper[:start], keepdims=True)
+                total = total + jnp.sum(lower * lower, keepdims=True)
+        copy = pltpu.make_async_copy(stat.at[s], stat_out.at[2 * block + s], sem_o.at[s])
+        copy.start()
+        stat_done.append(copy)
+        frob.append(jnp.sqrt(total + 1e-06))
+    eye = eye_tile(PANEL)
+    for s in range(2):
+        z = 2.5 / frob[s]
+        root0 = jnp.sqrt(jnp.sqrt(z)).astype(jnp.bfloat16).astype(jnp.float32)
+        for start, stop in panels(width):
+            for low, high in panels(width):
+                matrix = z * stat[s, low:high, start:stop]
+                factor = -0.25 * matrix
+                if low == start:
+                    factor = jnp.where(eye, 1.25, 0.0) + factor
+                factor = factor.astype(jnp.bfloat16)
+                mats[0, low:high, start:stop] = matrix.astype(jnp.bfloat16)
+                facs[0, low:high, start:stop] = factor
+                roots[s, 0, low:high, start:stop] = (root0 * factor.astype(jnp.float32)).astype(jnp.bfloat16)
+
+        def newton(it, carry):
+            cur, nxt = it, 1 - it
+            for start, stop in panels(width):
+                upper = dot_f32(facs[cur, :stop, :], facs[cur, :, start:stop])
+                store_symmetric(square, upper.astype(jnp.bfloat16), start, stop)
+            for start, stop in panels(width):
+                upper = dot_f32(square[:stop, :], square[:, start:stop])
+                store_symmetric(fourth, upper.astype(jnp.bfloat16), start, stop)
+            for start, stop in panels(width):
+                upper = dot_f32(fourth[:stop, :], mats[cur, :, start:stop])
+                store_symmetric(mats.at[nxt], upper.astype(jnp.bfloat16), start, stop)
+                diag = jnp.where(eye, 1.25, 0.0) - 0.25 * upper[start:]
+                facs[nxt, start:stop, start:stop] = diag.astype(jnp.bfloat16)
+                if start:
+                    off = (-0.25 * upper[:start]).astype(jnp.bfloat16)
+                    facs[nxt, :start, start:stop] = off
+                    facs[nxt, start:stop, :start] = off.T
+            for start, stop in panels(width):
+                upper = dot_f32(roots[s, cur, :stop, :], facs[nxt, :, start:stop])
+                store_symmetric(roots.at[s, nxt], upper.astype(jnp.bfloat16), start, stop)
+            return carry
+
+        lax.fori_loop(0, ITERS - 1, newton, 0)
+    last = (ITERS - 1) % 2
+    applied = square
+    for start, stop in panels(width):
+        applied[:, start:stop] = dot_f32(roots[0, last], grad[:, start:stop]).astype(jnp.bfloat16)
+    squares = jnp.zeros((1, 1), jnp.float32)
+    for start, stop in panels(width):
+        value = dot_f32(applied[...], roots[1, last, :, start:stop])
+        prod[:, start:stop] = value.astype(jnp.bfloat16)
+        squares = squares + jnp.sum(value * value, keepdims=True)
+    send = pltpu.make_async_copy(prod, prod_out, sem_p)
+    send.start()
+    squares_out[...] = jnp.broadcast_to(squares, squares_out.shape)
+    for copy in stat_done:
+        copy.wait()
+    send.wait()
+
+
+def block_call(block, scale, grad, statistics, carried):
+    width = grad.shape[-1]
+    square = (width, width)
+    any_spec = pl.BlockSpec(memory_space=pl.ANY)
+    operands = [scale, grad, statistics]
+    in_specs = [pl.BlockSpec(memory_space=pltpu.SMEM), any_spec, any_spec]
+    aliases = {}
+    if carried is not None:
+        aliases = {len(operands): 0}
+        operands.append(carried)
+        in_specs.append(any_spec)
+    flops = 2 * width ** 3 * 16
+    return pl.pallas_call(
+        functools.partial(block_kernel, block),
+        out_shape=(
+            jax.ShapeDtypeStruct(statistics.shape, jnp.float32),
+            jax.ShapeDtypeStruct(square, jnp.bfloat16),
+            jax.ShapeDtypeStruct((1, 128), jnp.float32),
+        ),
+        in_specs=in_specs,
+        out_specs=(any_spec, any_spec, pl.BlockSpec(memory_space=pltpu.VMEM)),
+        scratch_shapes=[
+            pltpu.VMEM(square, jnp.bfloat16),
+            pltpu.VMEM(square, jnp.bfloat16),
+            pltpu.VMEM((2,) + square, jnp.float32),
+            pltpu.VMEM((2,) + square, jnp.bfloat16),
+            pltpu.VMEM((2,) + square, jnp.bfloat16),
+            pltpu.VMEM((2, 2) + square, jnp.bfloat16),
+            pltpu.VMEM(square, jnp.bfloat16),
+            pltpu.VMEM(square, jnp.bfloat16),
+            pltpu.VMEM(square, jnp.bfloat16),
+            pltpu.SemaphoreType.DMA,
+            pltpu.SemaphoreType.DMA((2,)),
+            pltpu.SemaphoreType.DMA((2,)),
+            pltpu.SemaphoreType.DMA,
+        ],
+        input_output_aliases=aliases,
+        compiler_params=pltpu.CompilerParams(vmem_limit_bytes=56 * 1024 * 1024),
+        cost_estimate=pl.CostEstimate(flops=flops, bytes_accessed=20 * width * width, transcendentals=0),
+    )(*operands)
+
+
+def sum_everywhere(value, axes):
+    for axis in axes:
+        size = lax.axis_size(axis)
+        distance = 1
+        while distance < size:
+            value = value + lax.ppermute(value, axis, [(i, i ^ distance) for i in range(size)])
+            distance *= 2
+    return value
+
+
+def exchange(pieces):
+    return lax.all_to_all(pieces, "dp", split_axis=0, concat_axis=0, tiled=True)
+
+
+def on_device(gradients, statistics, accumulator):
+    owners = lax.axis_size("dp")
+    row_blocks, col_blocks, dev_rows, block_width = gradients.shape
+    blocks = row_blocks * col_blocks
+    chunks = statistics.shape[1] // 2
+    by_owner = gradients.reshape(owners, chunks, dev_rows, block_width)
+    grads_wide = gradients.astype(jnp.float32)
+    squares = jnp.full((1, 128), jnp.sum(grads_wide * grads_wide))
+    grad_total = sum_everywhere(squares, ("mp", "dp"))[0, 0]
+    entries = blocks * dev_rows * block_width * owners * lax.axis_size("mp")
+    clip_factor = jnp.minimum(1.0, jnp.sqrt(entries / (grad_total + 1e-06)))
+    scale = (0.1 / block_width * clip_factor * clip_factor).reshape(1)
+    wholes = []
+    for c in range(chunks):
+        whole = exchange(by_owner[:, c])
+        wholes.append(whole.reshape(block_width, block_width))
+    scaled = clip_factor * grads_wide
+    accumulated = accumulator + scaled * scaled
+    graft_step = scaled / jnp.sqrt(accumulated)
+    graft_squares = jnp.sum(graft_step * graft_step)
+    statistics_new = None
+    returned = []
+    update_squares = jnp.zeros((1, 128), jnp.float32)
+    for c in range(chunks):
+        statistics_new, product, part = block_call(c, scale, wholes[c], statistics[0], statistics_new)
+        update_squares = update_squares + part
+        returned.append(exchange(product.reshape(owners, dev_rows, block_width)))
+    lanes = lax.broadcasted_iota(jnp.int32, (1, 128), 1)
+    sums = jnp.where(lanes == 0, graft_squares, update_squares)
+    sums = sum_everywhere(sums, ("mp", "dp"))
+    graft_ratio = jnp.sqrt(sums[0, 0] / (sums[0, 1] + 1e-06))
+    update = graft_ratio * jnp.stack(returned, 1).astype(jnp.float32)
+    update = update.reshape(gradients.shape)
+    return (update, statistics_new[None], accumulated)
+
+
 def solution(mesh):
+    def run(gradients, statistics, accumulator):
+        if statistics.shape[1] % 2:
+            return on_device_plain(gradients, statistics, accumulator)
+        return on_device(gradients, statistics, accumulator)
+
     return jax.shard_map(
-        on_device,
+        run,
         mesh=mesh,
         in_specs=(P(None, "mp", "dp", None), P("mp", "dp", None, None), P(None, "mp", "dp", None)),
         out_specs=(P(None, "mp", "dp", None), P("mp", "dp", None, None), P(None, "mp", "dp", None)),

time: 487 us -> 336 us (0.69)
  the two profiles are of different devices: /device:TPU:12 before, /device:TPU:0 now
where the time goes in v1:
time: 336 us; the launch traced here: 334 us
  waiting for transfers between devices  108 us (32%)
  Pallas kernels  106 us (32%)
  blocking collectives  52 us (15%)
  starting transfers between devices  36.2 us (11%)
  other arithmetic  18.1 us (5%)
  local copies, waits for them, and re-layouts  10.3 us (3%)
    pallas_call x2, Pallas kernels, block_call(): pl.pallas_call(functools.partial(block_kernel, block), out_shape=(jax.Sha...  106 us
    ppermute x10, waiting for transfers between devices, sum_everywhere(): lax.ppermute(value, axis, [(i, i ^ distance) for i in range(size)])  65.6 us
    all_to_all x1, blocking collectives, exchange(): return lax.all_to_all(pieces, 'dp', split_axis=0, concat_axis=0, tiled=True)  52 us
    all_to_all x3, waiting for transfers between devices, exchange(): return lax.all_to_all(pieces, 'dp', split_axis=0, concat_axis=0, tiled=True)  42.6 us
    ppermute x10, starting transfers between devices, sum_everywhere(): lax.ppermute(value, axis, [(i, i ^ distance) for i in range(size)])  19.1 us
    all_to_all x3, starting transfers between devices, exchange(): return lax.all_to_all(pieces, 'dp', split_axis=0, concat_axis=0, tiled=True)  17.1 us
    reduce_sum x1, other arithmetic, on_device(): graft_squares = jnp.sum(graft_step * graft_step)  8.41 us
  transfers between devices with their start and end apart: 13, of which 10 were waited for; matrix products, arithmetic and copies ran while one was open for 5% of the time, Pallas kernels for 16%

profile of v1, /device:TPU:0, one launch (start us, length us, event | category | flops | bytes accessed | tf_op | source)
XLA Modules:
  0.0 333.7 jit_solution(1493113669002032244)
XLA Ops:
  0.6 4.8 %slice_bitcast_fusion.1 = (bf16[8,128,1024]{2,1,0:T(8,128)(2,1)}, bf16[8,128,1024]{2,1,0:T(8,128)(2,1)}) fusion(bf16[8,2,128,1024]{3,2,1,0:T(8,128)(2,1)} %bitcast.22), kind=kLoop, calls=%fused_computation.10 | loop fusion | bytes 8388608 | tf_op jit(solution)/shard_map/squeeze | solution.py:295
  5.5 7.3 %all-to-all-start = ((bf16[8,128,1024]{2,1,0:T(8,128)(2,1)}), bf16[8,128,1024]{2,1,0:T(8,128)(2,1)S(1)}, u32[]{:S(2)}, u32[]{:S(2)}) async-start(bf16[8,128,1024]{2,1,0:T(8,128)(2,1)} %get-tuple-element.17), calls=%async_computation | async-start | bytes 4194304 | tf_op jit(solution)/shard_map/all_to_all | solution.py:278
  12.8 4.9 %fusion.5 = f32[]{:T(128)} fusion(bf16[4,4,128,1024]{3,2,1,0:T(8,128)(2,1)} %param.3), kind=kLoop, calls=%fused_computation.7 | loop fusion | flops 6291455 | bytes 4194308 | tf_op jit(solution)/shard_map/reduce_sum | solution.py:288
  18.5 42.6 %all-to-all-done = bf16[8,128,1024]{2,1,0:T(8,128)(2,1)S(1)} async-done(((bf16[8,128,1024]{2,1,0:T(8,128)(2,1)}), bf16[8,128,1024]{2,1,0:T(8,128)(2,1)S(1)}, u32[]{:S(2)}, u32[]{:S(2)}) %all-to-all-start) | async-done | bytes 2097184 | tf_op jit(solution)/shard_map/all_to_all | solution.py:278
  61.0 4.9 %all-to-all-start.1 = ((bf16[8,128,1024]{2,1,0:T(8,128)(2,1)}), bf16[8,128,1024]{2,1,0:T(8,128)(2,1)}, u32[]{:S(2)}, u32[]{:S(2)}) async-start(bf16[8,128,1024]{2,1,0:T(8,128)(2,1)} %get-tuple-element.18), calls=%async_computation.1 | async-start | bytes 4194304 | tf_op jit(solution)/shard_map/all_to_all | solution.py:278
  68.2 2.1 collective-permute-done.1
  70.9 2.0 collective-permute-start.2
  73.0 9.6 %collective-permute-done.2 = f32[1,128]{1,0:T(1,128)S(1)} collective-permute-done((f32[1,128]{1,0:T(1,128)S(1)}, f32[1,128]{1,0:T(1,128)S(1)}, u32[]{:S(2)}, u32[]{:S(2)}) %collective-permute-start.2) | collective-permute-done | bytes 544 | tf_op jit(solution)/shard_map/ppermute | solution.py:272
  84.3 15.8 %collective-permute-done.3 = f32[1,128]{1,0:T(1,128)S(1)} collective-permute-done((f32[1,128]{1,0:T(1,128)S(1)}, f32[1,128]{1,0:T(1,128)S(1)}, u32[]{:S(2)}, u32[]{:S(2)}) %collective-permute-start.3) | collective-permute-done | bytes 544 | tf_op jit(solution)/shard_map/ppermute | solution.py:272
  100.1 3.9 %collective-permute-start.4 = (f32[1,128]{1,0:T(1,128)S(1)}, f32[1,128]{1,0:T(1,128)S(1)}, u32[]{:S(2)}, u32[]{:S(2)}) collective-permute-start(f32[1,128]{1,0:T(1,128)S(1)} %add.47), channel_id=1, source_target_pairs={{0,16},{4,20},{8,24},{12,28},{16,0},{20,4},{24,8},{28,12},{1,17},{... | collective-permute-start | bytes 1544 | tf_op jit(solution)/shard_map/ppermute | solution.py:272
  104.0 9.8 %collective-permute-done.4 = f32[1,128]{1,0:T(1,128)S(1)} collective-permute-done((f32[1,128]{1,0:T(1,128)S(1)}, f32[1,128]{1,0:T(1,128)S(1)}, u32[]{:S(2)}, u32[]{:S(2)}) %collective-permute-start.4) | collective-permute-done | bytes 544 | tf_op jit(solution)/shard_map/ppermute | solution.py:272
  113.9 53.1 %shard_map.58 = (f32[4,1024,1024]{2,1,0:T(8,128)}, bf16[1024,1024]{1,0:T(8,128)(2,1)}, f32[1,128]{1,0:T(1,128)}) custom-call(f32[1]{0:T(128)} %bitcast.1.scale_ref, bf16[1024,1024]{1,0:T(8,128)(2,1)} %bitcast.26, f32[4,1024,1024]{2,1,0:T(8,128)} %bitcast.28), custom_call_target="tpu_custom_call" | custom-call | flops 34359738368 | bytes 20971520 | tf_op jit(solution)/shard_map/pallas_call | solution.py:237
  167.1 53.3 %shard_map.59 = (f32[4,1024,1024]{2,1,0:T(8,128)}, bf16[1024,1024]{1,0:T(8,128)(2,1)}, f32[1,128]{1,0:T(1,128)}) custom-call(f32[1]{0:T(128)} %bitcast.1.scale_ref, bf16[1024,1024]{1,0:T(8,128)(2,1)} %bitcast.7.grad_hbm, f32[4,1024,1024]{2,1,0:T(8,128)} %bitcast.29, f32[4,1024,1024]{2,1,0:T(8,128)} %get-tuple-element.10.rest_0_), custom_call_target="tpu_custom_call", output_to_operand_aliasing={{0}: (3, {})} | custom-call | flops 34359738368 | bytes 20971520 | tf_op jit(solution)/shard_map/pallas_call | solution.py:237
  220.4 52.0 %all_to_all.20 = bf16[8,128,1024]{2,1,0:T(8,128)(2,1)S(1)} all-to-all(bf16[8,128,1024]{2,1,0:T(8,128)(2,1)} %bitcast.27), channel_id=1, replica_groups=mesh['dp'=8,'mp'=4] {'dp'}, dimensions={0} | all-to-all | bytes 4194304 | tf_op jit(solution)/shard_map/all_to_all | solution.py:278
  272.4 4.9 %all-to-all-start.2 = ((bf16[8,128,1024]{2,1,0:T(8,128)(2,1)}), bf16[8,128,1024]{2,1,0:T(8,128)(2,1)}, u32[]{:S(2)}, u32[]{:S(2)}) async-start(bf16[8,128,1024]{2,1,0:T(8,128)(2,1)} %bitcast.25), calls=%async_computation.2 | async-start | bytes 4194304 | tf_op jit(solution)/shard_map/all_to_all | solution.py:278
  277.3 8.4 %fusion.4 = (f32[]{:T(128)}, f32[4,4,128,1024]{3,2,1,0:T(8,128)}) fusion(bf16[4,4,128,1024]{3,2,1,0:T(8,128)(2,1)} %param.3, f32[]{:T(128)} %bitcast, f32[4,4,128,1024]{3,2,1,0:T(8,128)} %param.5), kind=kLoop, calls=%fused_computation.6 | loop fusion | flops 14680063 | bytes 20971528 | tf_op jit(solution)/shard_map/reduce_sum | solution.py:300
  289.1 2.1 collective-permute-done.6
  291.2 2.0 collective-permute-start.7
  294.8 2.0 collective-permute-start.8
  296.7 13.7 %collective-permute-done.8 = f32[1,128]{1,0:T(1,128)S(1)} collective-permute-done((f32[1,128]{1,0:T(1,128)S(1)}, f32[1,128]{1,0:T(1,128)S(1)}, u32[]{:S(2)}, u32[]{:S(2)}) %collective-permute-start.8) | collective-permute-done | bytes 544 | tf_op jit(solution)/shard_map/ppermute | solution.py:272
  310.5 4.4 %collective-permute-start.9 = (f32[1,128]{1,0:T(1,128)S(1)}, f32[1,128]{1,0:T(1,128)S(1)}, u32[]{:S(2)}, u32[]{:S(2)}) collective-permute-start(f32[1,128]{1,0:T(1,128)S(1)} %add.55), channel_id=1, source_target_pairs={{0,16},{4,20},{8,24},{12,28},{16,0},{20,4},{24,8},{28,12},{1,17},{... | collective-permute-start | bytes 1544 | tf_op jit(solution)/shard_map/ppermute | solution.py:272
  314.8 9.8 %collective-permute-done.9 = f32[1,128]{1,0:T(1,128)S(1)} collective-permute-done((f32[1,128]{1,0:T(1,128)S(1)}, f32[1,128]{1,0:T(1,128)S(1)}, u32[]{:S(2)}, u32[]{:S(2)}) %collective-permute-start.9) | collective-permute-done | bytes 544 | tf_op jit(solution)/shard_map/ppermute | solution.py:272
  326.5 2.8 convert_multiply_fusion.2
  329.3 4.2 %copy.9 = f32[8,2,128,1024]{3,2,1,0:T(8,128)} copy(f32[8,2,128,1024]{3,2,0,1:T(8,128)S(1)} %convert_multiply_fusion.2) | data formatting | bytes 16777216 | tf_op jit(solution)/shard_map/mul | solution.py:312
  (29 shorter events, 10.9 us)
Async XLA Ops:
  5.5 55.5 %all-to-all-start = ((bf16[8,128,1024]{2,1,0:T(8,128)(2,1)}), bf16[8,128,1024]{2,1,0:T(8,128)(2,1)S(1)}, u32[]{:S(2)}, u32[]{:S(2)}) async-start(bf16[8,128,1024]{2,1,0:T(8,128)(2,1)} %get-tuple-element.17), calls=%async_computation | async-start | bytes 4194304 | tf_op jit(solution)/shard_map/all_to_all | solution.py:278
  18.4 47.6 %collective-permute-start = (f32[1,128]{1,0:T(1,128)S(1)}, f32[1,128]{1,0:T(1,128)S(1)}, u32[]{:S(2)}, u32[]{:S(2)}) collective-permute-start(f32[1,128]{1,0:T(1,128)S(1)} %broadcast_in_dim.10), channel_id=1, source_target_pairs={{0,1},{1,0},{2,3},{3,2},{4,5},{5,4},{6,7},{7,6},{8,9},{9,8},{10,11... | collective-permute-start | bytes 1544 | tf_op jit(solution)/shard_map/ppermute | solution.py:272
  61.0 52.9 %copy-start = (bf16[8,128,1024]{2,1,0:T(8,128)(2,1)}, bf16[8,128,1024]{2,1,0:T(8,128)(2,1)S(1)}, u32[]{:S(2)}) copy-start(bf16[8,128,1024]{2,1,0:T(8,128)(2,1)S(1)} %all-to-all-done) | copy-start | bytes 6291460
  61.0 106.1 %all-to-all-start.1 = ((bf16[8,128,1024]{2,1,0:T(8,128)(2,1)}), bf16[8,128,1024]{2,1,0:T(8,128)(2,1)}, u32[]{:S(2)}, u32[]{:S(2)}) async-start(bf16[8,128,1024]{2,1,0:T(8,128)(2,1)} %get-tuple-element.18), calls=%async_computation.1 | async-start | bytes 4194304 | tf_op jit(solution)/shard_map/all_to_all | solution.py:278
  66.6 3.6 %collective-permute-start.1 = (f32[1,128]{1,0:T(1,128)S(1)}, f32[1,128]{1,0:T(1,128)S(1)}, u32[]{:S(2)}, u32[]{:S(2)}) collective-permute-start(f32[1,128]{1,0:T(1,128)S(1)} %broadcast_add_fusion), channel_id=1, source_target_pairs={{0,2},{1,3},{2,0},{3,1},{4,6},{5,7},{6,4},{7,5},{8,10},{9,11},{10,... | collective-permute-start | bytes 1544 | tf_op jit(solution)/shard_map/ppermute | solution.py:272
  70.9 11.7 %collective-permute-start.2 = (f32[1,128]{1,0:T(1,128)S(1)}, f32[1,128]{1,0:T(1,128)S(1)}, u32[]{:S(2)}, u32[]{:S(2)}) collective-permute-start(f32[1,128]{1,0:T(1,128)S(1)} %fusion.8), channel_id=1, source_target_pairs={{0,4},{4,0},{8,12},{12,8},{16,20},{20,16},{24,28},{28,24},{1,5},{5... | collective-permute-start | bytes 1544 | tf_op jit(solution)/shard_map/ppermute | solution.py:272
  82.6 17.5 %collective-permute-start.3 = (f32[1,128]{1,0:T(1,128)S(1)}, f32[1,128]{1,0:T(1,128)S(1)}, u32[]{:S(2)}, u32[]{:S(2)}) collective-permute-start(f32[1,128]{1,0:T(1,128)S(1)} %add.46), channel_id=1, source_target_pairs={{0,8},{4,12},{8,0},{12,4},{16,24},{20,28},{24,16},{28,20},{1,9},{5... | collective-permute-start | bytes 1544 | tf_op jit(solution)/shard_map/ppermute | solution.py:272
  100.1 13.7 %collective-permute-start.4 = (f32[1,128]{1,0:T(1,128)S(1)}, f32[1,128]{1,0:T(1,128)S(1)}, u32[]{:S(2)}, u32[]{:S(2)}) collective-permute-start(f32[1,128]{1,0:T(1,128)S(1)} %add.47), channel_id=1, source_target_pairs={{0,16},{4,20},{8,24},{12,28},{16,0},{20,4},{24,8},{28,12},{1,17},{... | collective-permute-start | bytes 1544 | tf_op jit(solution)/shard_map/ppermute | solution.py:272
  272.4 54.1 %all-to-all-start.2 = ((bf16[8,128,1024]{2,1,0:T(8,128)(2,1)}), bf16[8,128,1024]{2,1,0:T(8,128)(2,1)}, u32[]{:S(2)}, u32[]{:S(2)}) async-start(bf16[8,128,1024]{2,1,0:T(8,128)(2,1)} %bitcast.25), calls=%async_computation.2 | async-start | bytes 4194304 | tf_op jit(solution)/shard_map/all_to_all | solution.py:278
  277.3 8.4 %copy-start.1 = (f32[1,128]{1,0:T(1,128)S(1)}, f32[1,128]{1,0:T(1,128)}, u32[]{:S(2)}) copy-start(f32[1,128]{1,0:T(1,128)} %get-tuple-element.9) | copy-start | bytes 1540
  277.3 8.4 %copy-start.2 = (f32[1,128]{1,0:T(1,128)S(1)}, f32[1,128]{1,0:T(1,128)}, u32[]{:S(2)}) copy-start(f32[1,128]{1,0:T(1,128)} %get-tuple-element.11) | copy-start | bytes 1540
  286.4 1.2 collective-permute-start.5
  287.6 3.6 %collective-permute-start.6 = (f32[1,128]{1,0:T(1,128)S(1)}, f32[1,128]{1,0:T(1,128)S(1)}, u32[]{:S(2)}, u32[]{:S(2)}) collective-permute-start(f32[1,128]{1,0:T(1,128)S(1)} %add.52), channel_id=1, source_target_pairs={{0,2},{1,3},{2,0},{3,1},{4,6},{5,7},{6,4},{7,5},{8,10},{9,11},{10,... | collective-permute-start | bytes 1544 | tf_op jit(solution)/shard_map/ppermute | solution.py:272
  291.2 3.6 %collective-permute-start.7 = (f32[1,128]{1,0:T(1,128)S(1)}, f32[1,128]{1,0:T(1,128)S(1)}, u32[]{:S(2)}, u32[]{:S(2)}) collective-permute-start(f32[1,128]{1,0:T(1,128)S(1)} %add.53), channel_id=1, source_target_pairs={{0,4},{4,0},{8,12},{12,8},{16,20},{20,16},{24,28},{28,24},{1,5},{5... | collective-permute-start | bytes 1544 | tf_op jit(solution)/shard_map/ppermute | solution.py:272
  294.8 15.7 %collective-permute-start.8 = (f32[1,128]{1,0:T(1,128)S(1)}, f32[1,128]{1,0:T(1,128)S(1)}, u32[]{:S(2)}, u32[]{:S(2)}) collective-permute-start(f32[1,128]{1,0:T(1,128)S(1)} %add.54), channel_id=1, source_target_pairs={{0,8},{4,12},{8,0},{12,4},{16,24},{20,28},{24,16},{28,20},{1,9},{5... | collective-permute-start | bytes 1544 | tf_op jit(solution)/shard_map/ppermute | solution.py:272
  310.5 14.1 %collective-permute-start.9 = (f32[1,128]{1,0:T(1,128)S(1)}, f32[1,128]{1,0:T(1,128)S(1)}, u32[]{:S(2)}, u32[]{:S(2)}) collective-permute-start(f32[1,128]{1,0:T(1,128)S(1)} %add.55), channel_id=1, source_target_pairs={{0,16},{4,20},{8,24},{12,28},{16,0},{20,4},{24,8},{28,12},{1,17},{... | collective-permute-start | bytes 1544 | tf_op jit(solution)/shard_map/ppermute | solution.py:272

commit v2 on v0

--- a/solution.py
+++ b/solution.py
@@ -1,9 +1,15 @@
+import functools
+
 import jax
 import jax.numpy as jnp
 from jax import lax
+from jax.experimental import pallas as pl
+from jax.experimental.pallas import tpu as pltpu
 from jax.sharding import PartitionSpec as P
 
+
 ITERS = 3
+PANEL = 256
 
 
 def partner_2(value, axis, distance):
@@ -31,7 +37,7 @@
     return root_iter
 
 
-def on_device(gradients, statistics, accumulator):
+def on_device_plain(gradients, statistics, accumulator):
     owners = lax.axis_size("dp")
     own_index = lax.axis_index("dp")
     row_blocks, col_blocks, dev_rows, block_width = gradients.shape
@@ -108,9 +114,351 @@
     return (graft_ratio * returned, statistics_new[None], accumulated)
 
 
+def dot_f32(left, right):
+    return jnp.dot(left, right, preferred_element_type=jnp.float32)
+
+
+def panels(width):
+    return [(start, start + PANEL) for start in range(0, width, PANEL)]
+
+
+def lane_sums(value):
+    return jnp.sum(value.reshape(-1, 8, value.shape[-1]), axis=0)
+
+
+def mirrored(left, right, out, post=None):
+    for start, stop in panels(left.shape[0]):
+        value = dot_f32(left[:stop, :], right[:, start:stop])
+        upper = value.astype(jnp.bfloat16)
+        out[:stop, start:stop] = upper
+        if start:
+            out[start:stop, :start] = upper[:start].T
+        if post is not None:
+            post(value, start, stop)
+
+
+def block_kernel(block, partners, whole, me_ref, scale_ref, own_hbm, stat_hbm, *rest):
+    received = rest[: len(partners)]
+    outs = rest[len(rest) - 17 - (0 if whole else len(partners)):]
+    stat_out = outs[0]
+    prod_outs = outs[1 : len(outs) - 15]
+    (squares_out,
+     grads, stat_old, stat, matrix, factor, root, square, fourth, left_root, sums,
+     sem_g, sem_s, sem_o, sem_p) = outs[len(outs) - 15:]
+    width = grads.shape[1]
+    dev_rows = own_hbm.shape[2]
+    me = me_ref[0]
+
+    def rows_of(partner):
+        return pl.ds(pl.multiple_of((me ^ partner) * dev_rows, dev_rows), dev_rows)
+
+    grad_in = [pltpu.make_async_copy(own_hbm.at[me, block], grads.at[0, rows_of(0), :], sem_g.at[0])]
+    for n, partner in enumerate(partners):
+        grad_in.append(pltpu.make_async_copy(received[n], grads.at[0, rows_of(partner), :], sem_g.at[n + 1]))
+    for copy in grad_in:
+        copy.start()
+    stat_in = pltpu.make_async_copy(stat_hbm.at[pl.ds(2 * block, 2)], stat_old, sem_s)
+    stat_in.start()
+    for copy in grad_in:
+        copy.wait()
+    scale = scale_ref[0]
+    tile = (PANEL, PANEL)
+    eye = lax.broadcasted_iota(jnp.int32, tile, 0) == lax.broadcasted_iota(jnp.int32, tile, 1)
+    bias = jnp.where(eye, 1.25, 0.0)
+    for start, stop in panels(width):
+        grads[1, :, start:stop] = grads[0, start:stop, :].T
+    stat_in.wait()
+
+    def gram_step(s, carry):
+        total = jnp.zeros((8, PANEL), jnp.float32)
+        for start, stop in panels(width):
+            gram = scale * dot_f32(grads[s, :stop, :], grads[1 - s, :, start:stop])
+            upper = 0.9 * stat_old[s, :stop, start:stop] + gram
+            stat[s, :stop, start:stop] = upper
+            total = total + lane_sums(upper * upper)
+            for low in range(0, start, PANEL):
+                high = low + PANEL
+                lower = 0.9 * stat_old[s, start:stop, low:high] + gram[low:high].T
+                stat[s, start:stop, low:high] = lower
+                total = total + lane_sums(lower * lower)
+        sums[s] = total
+        return carry
+
+    lax.fori_loop(0, 2, gram_step, 0)
+    stat_done = pltpu.make_async_copy(stat, stat_out.at[pl.ds(2 * block, 2)], sem_o)
+    stat_done.start()
+
+    def root_step(s, carry):
+        left_root[...] = root[...]
+        z = 2.5 / jnp.sqrt(jnp.sum(sums[s], keepdims=True) + 1e-06)
+        root0 = jnp.sqrt(jnp.sqrt(z)).astype(jnp.bfloat16).astype(jnp.float32)
+        for start, stop in panels(width):
+            for low, high in panels(width):
+                scaled = z * stat[s, low:high, start:stop]
+                first = -0.25 * scaled
+                if low == start:
+                    first = bias + first
+                first = first.astype(jnp.bfloat16)
+                matrix[low:high, start:stop] = scaled.astype(jnp.bfloat16)
+                factor[low:high, start:stop] = first
+                root[low:high, start:stop] = (root0 * first.astype(jnp.float32)).astype(jnp.bfloat16)
+
+        def next_factor(value, start, stop):
+            factor[start:stop, start:stop] = (bias - 0.25 * value[start:]).astype(jnp.bfloat16)
+            if start:
+                off = (-0.25 * value[:start]).astype(jnp.bfloat16)
+                factor[:start, start:stop] = off
+                factor[start:stop, :start] = off.T
+
+        def newton(it, inner):
+            mirrored(factor, factor, square)
+            mirrored(square, square, fourth)
+            mirrored(fourth, matrix, matrix, next_factor)
+            mirrored(factor, root, root)
+            return inner
+
+        lax.fori_loop(0, ITERS - 1, newton, 0)
+        return carry
+
+    lax.fori_loop(0, 2, root_step, 0)
+    for start, stop in panels(width):
+        square[:, start:stop] = dot_f32(left_root[...], grads[0, :, start:stop]).astype(jnp.bfloat16)
+    total = jnp.zeros((8, PANEL), jnp.float32)
+    for start, stop in panels(width):
+        value = dot_f32(square[...], root[:, start:stop])
+        fourth[:, start:stop] = value.astype(jnp.bfloat16)
+        total = total + lane_sums(value * value)
+    if whole:
+        sends = [pltpu.make_async_copy(fourth, prod_outs[0], sem_p.at[0])]
+    else:
+        sends = [
+            pltpu.make_async_copy(fourth.at[rows_of(partner), :], prod_outs[n], sem_p.at[n])
+            for n, partner in enumerate((0, *partners))
+        ]
+    for send in sends:
+        send.start()
+    squares_out[...] = jnp.broadcast_to(jnp.sum(total, keepdims=True), squares_out.shape)
+    stat_done.wait()
+    for send in sends:
+        send.wait()
+
+
+def block_call(block, partners, whole, me, scale, own, received, statistics, carried):
+    dev_rows, width = own.shape[2:]
+    square = (width, width)
+    hbm = pl.BlockSpec(memory_space=pltpu.HBM)
+    smem = pl.BlockSpec(memory_space=pltpu.SMEM)
+    operands = [me, scale, own, statistics, *received]
+    in_specs = [smem, smem] + [hbm] * (2 + len(received))
+    aliases = {}
+    if carried is not None:
+        aliases = {len(operands): 0}
+        operands.append(carried)
+        in_specs.append(hbm)
+    pieces = 1 if whole else len(partners) + 1
+    piece_shape = square if whole else (dev_rows, width)
+    flops = 2 * width ** 3 * 16
+    results = pl.pallas_call(
+        functools.partial(block_kernel, block, partners, whole),
+        out_shape=(
+            jax.ShapeDtypeStruct(statistics.shape, jnp.float32),
+            *[jax.ShapeDtypeStruct(piece_shape, jnp.bfloat16) for _ in range(pieces)],
+            jax.ShapeDtypeStruct((1, 128), jnp.float32),
+        ),
+        in_specs=in_specs,
+        out_specs=(hbm, *[hbm] * pieces, pl.BlockSpec(memory_space=pltpu.VMEM)),
+        scratch_shapes=[
+            pltpu.VMEM((2,) + square, jnp.bfloat16),
+            pltpu.VMEM((2,) + square, jnp.float32),
+            pltpu.VMEM((2,) + square, jnp.float32),
+            *[pltpu.VMEM(square, jnp.bfloat16) for _ in range(6)],
+            pltpu.VMEM((2, 8, PANEL), jnp.float32),
+            pltpu.SemaphoreType.DMA((len(partners) + 1,)),
+            pltpu.SemaphoreType.DMA,
+            pltpu.SemaphoreType.DMA,
+            pltpu.SemaphoreType.DMA((len(partners) + 1,)),
+        ],
+        input_output_aliases=aliases,
+        compiler_params=pltpu.CompilerParams(vmem_limit_bytes=58 * 1024 * 1024),
+        cost_estimate=pl.CostEstimate(flops=flops, bytes_accessed=20 * width * width, transcendentals=0),
+    )(*operands)
+    return results[0], results[1:-1], results[-1]
+
+
+def scale_rows(ratio_ref, rows_ref, *rest):
+    out_ref = rest[-1]
+    out_ref[...] = ratio_ref[0] * rows_ref[...].astype(jnp.float32)
+
+
+def scale_whole(chunk, chunks, ratio, rows, carried):
+    owners, dev_rows, width = rows.shape
+    step = max(1, owners // 4)
+    operands = [ratio, rows]
+    in_specs = [
+        pl.BlockSpec(memory_space=pltpu.SMEM),
+        pl.BlockSpec((step, dev_rows, width), lambda i: (i, 0, 0)),
+    ]
+    aliases = {}
+    if carried is not None:
+        aliases = {len(operands): 0}
+        operands.append(carried)
+        in_specs.append(pl.BlockSpec(memory_space=pltpu.HBM))
+    return pl.pallas_call(
+        scale_rows,
+        grid=(owners // step,),
+        out_shape=jax.ShapeDtypeStruct((owners, chunks, dev_rows, width), jnp.float32),
+        in_specs=in_specs,
+        out_specs=pl.BlockSpec((step, None, dev_rows, width), lambda i: (i, chunk, 0, 0)),
+        input_output_aliases=aliases,
+        compiler_params=pltpu.CompilerParams(vmem_limit_bytes=16 * 1024 * 1024),
+        cost_estimate=pl.CostEstimate(flops=rows.size, bytes_accessed=6 * rows.size, transcendentals=0),
+    )(*operands)
+
+
+def scale_kernel(chunk, partners, me_ref, ratio_ref, *rest):
+    count = len(partners) + 1
+    pieces = rest[:count]
+    out_ref, narrow, wide, sem_in, sem_out = rest[-5:]
+    me = me_ref[0]
+    loads = [pltpu.make_async_copy(pieces[n], narrow.at[n], sem_in.at[n]) for n in range(count)]
+    for load in loads:
+        load.start()
+    stores = []
+    for n, partner in enumerate((0, *partners)):
+        loads[n].wait()
+        wide[n] = ratio_ref[0] * narrow[n].astype(jnp.float32)
+        store = pltpu.make_async_copy(wide.at[n], out_ref.at[me ^ partner, chunk], sem_out.at[n])
+        store.start()
+        stores.append(store)
+    for store in stores:
+        store.wait()
+
+
+def scale_pieces(chunk, chunks, partners, me, ratio, pieces, carried):
+    dev_rows, width = pieces[0].shape
+    owners = len(pieces)
+    hbm = pl.BlockSpec(memory_space=pltpu.HBM)
+    smem = pl.BlockSpec(memory_space=pltpu.SMEM)
+    operands = [me, ratio, *pieces]
+    in_specs = [smem, smem] + [hbm] * owners
+    aliases = {}
+    if carried is not None:
+        aliases = {len(operands): 0}
+        operands.append(carried)
+        in_specs.append(hbm)
+    size = owners * dev_rows * width
+    return pl.pallas_call(
+        functools.partial(scale_kernel, chunk, partners),
+        out_shape=jax.ShapeDtypeStruct((owners, chunks, dev_rows, width), jnp.float32),
+        in_specs=in_specs,
+        out_specs=hbm,
+        scratch_shapes=[
+            pltpu.VMEM((owners, dev_rows, width), jnp.bfloat16),
+            pltpu.VMEM((owners, dev_rows, width), jnp.float32),
+            pltpu.SemaphoreType.DMA((owners,)),
+            pltpu.SemaphoreType.DMA((owners,)),
+        ],
+        input_output_aliases=aliases,
+        compiler_params=pltpu.CompilerParams(vmem_limit_bytes=16 * 1024 * 1024),
+        cost_estimate=pl.CostEstimate(flops=size, bytes_accessed=6 * size, transcendentals=0),
+    )(*operands)
+
+
+def partner_order(owners):
+    half = owners // 2
+    order = (owners - 2, *range(2, half), owners - 1, *range(half, owners - 2), 1)
+    return tuple(dict.fromkeys(d for d in order if 0 < d < owners))
+
+
+def swap(piece, partner):
+    size = lax.axis_size("dp")
+    return lax.ppermute(piece, "dp", [(i, i ^ partner) for i in range(size)])
+
+
+def sum_over(value, axis):
+    size = lax.axis_size(axis)
+    parts = [
+        lax.ppermute(value, axis, [(i, (i + shift) % size) for i in range(size)])
+        for shift in range(1, size)
+    ]
+    for part in parts:
+        value = value + part
+    return value
+
+
+def exchange(pieces):
+    return lax.all_to_all(pieces, "dp", split_axis=0, concat_axis=0, tiled=True)
+
+
+def on_device(gradients, statistics, accumulator):
+    owners = lax.axis_size("dp")
+    row_blocks, col_blocks, dev_rows, block_width = gradients.shape
+    blocks = row_blocks * col_blocks
+    chunks = statistics.shape[1] // 2
+    by_owner = gradients.reshape(owners, chunks, dev_rows, block_width)
+    grads_wide = gradients.astype(jnp.float32)
+    squares = jnp.full((1, 128), jnp.sum(grads_wide * grads_wide))
+    partners = partner_order(owners)
+    own_index = lax.axis_index("dp")
+    me = own_index.astype(jnp.int32).reshape(1)
+    received = []
+    source = by_owner
+    for c in range(chunks):
+        parts = []
+        for partner in partners:
+            piece = lax.dynamic_slice(
+                source, (own_index ^ partner, c, 0, 0), (1, 1, dev_rows, block_width)
+            )
+            source, piece = lax.optimization_barrier((source, piece))
+            parts.append(swap(piece.reshape(dev_rows, block_width), partner))
+        received.append(parts)
+    grad_total = sum_over(squares, "mp")
+    grad_total = sum_over(grad_total, "dp")[0, 0]
+    entries = blocks * dev_rows * block_width * owners * lax.axis_size("mp")
+    clip_factor = jnp.minimum(1.0, jnp.sqrt(entries / (grad_total + 1e-06)))
+    scale = (0.1 / block_width * clip_factor * clip_factor).reshape(1)
+    scaled = clip_factor * grads_wide
+    accumulated = accumulator + scaled * scaled
+    graft_step = scaled / jnp.sqrt(accumulated)
+    graft_squares = jnp.sum(graft_step * graft_step)
+    statistics_new = None
+    returned = []
+    update_squares = jnp.zeros((1, 128), jnp.float32)
+    for c in range(chunks):
+        whole = c + 1 < chunks
+        statistics_new, product, part = block_call(
+            c, partners, whole, me, scale, by_owner, received[c], statistics[0], statistics_new
+        )
+        update_squares = update_squares + part
+        if whole:
+            returned.append(exchange(product[0].reshape(owners, dev_rows, block_width)))
+        else:
+            parts = [product[0]]
+            for n, partner in enumerate(partners):
+                parts.append(swap(product[n + 1], partner))
+            returned.append(parts)
+    lanes = lax.broadcasted_iota(jnp.int32, (1, 128), 1)
+    sums = jnp.where(lanes == 0, graft_squares, update_squares)
+    sums = sum_over(sums, "mp")
+    sums = sum_over(sums, "dp")
+    graft_ratio = jnp.sqrt(sums[0, :1] / (sums[0, 1:2] + 1e-06))
+    update = None
+    for c in range(chunks):
+        if c + 1 < chunks:
+            update = scale_whole(c, chunks, graft_ratio, returned[c], update)
+        else:
+            update = scale_pieces(c, chunks, partners, me, graft_ratio, returned[c], update)
+    return (update.reshape(gradients.shape), statistics_new[None], accumulated)
+
+
 def solution(mesh):
+    def run(gradients, statistics, accumulator):
+        if statistics.shape[1] != 4:
+            return on_device_plain(gradients, statistics, accumulator)
+        return on_device(gradients, statistics, accumulator)
+
     return jax.shard_map(
-        on_device,
+        run,
         mesh=mesh,
         in_specs=(P(None, "mp", "dp", None), P("mp", "dp", None, None), P(None, "mp", "dp", None)),
         out_specs=(P(None, "mp", "dp", None), P("mp", "dp", None, None), P(None, "mp", "dp", None)),

time: 487 us -> 282 us (0.58)
  matrix products: 179 us -> 0 us
  blocking collectives: 151 us -> 0 us
  Pallas kernels: 0 us -> 91.7 us
  starting transfers between devices: 12.8 us -> 71.5 us
  other arithmetic: 36.4 us -> 14.2 us
  local copies, waits for them, and re-layouts: 23.8 us -> 15.2 us
    dot_general x8 -> x0, matrix products: 179 us -> none  [the longest x7 156 us: batch_dot(): jnp.einsum('kij,kjl->kil', left, right, preferred_element_type=jnp.float32)]
    psum x2 -> x0, blocking collectives: 151 us -> none  [the longest x1 107 us: on_device(): grad_total = lax.psum(jnp.sum(grads_wide * grads_wide), ('dp', 'mp'))]
    pallas_call x0 -> x4, Pallas kernels: none -> 91.7 us  [the longest x2 86.9 us: block_call(): pl.pallas_call(functools.partial(block_kernel, block, partners, whole), o...]
    ppermute x0 -> x41, waiting for transfers between devices: none -> 81.5 us  [the longest x21 46 us: swap(): return lax.ppermute(piece, 'dp', [(i, i ^ partner) for i in range(size)])]
    all_to_all x2 -> x1, waiting for transfers between devices: 80.1 us -> 0.01 us  [exchange(): return lax.all_to_all(pieces, 'dp', split_axis=0, concat_axis=0, tiled=True)]
    ppermute x0 -> x41, starting transfers between devices: none -> 67.2 us  [the longest x21 38.7 us: swap(): return lax.ppermute(piece, 'dp', [(i, i ^ partner) for i in range(size)])]
    all_to_all x3 -> x0, local copies, waits for them, and re-layouts: 19 us -> none  [on_device(): lax.all_to_all(row_units, 'dp', split_axis=0, concat_axis=1, tiled=True)]
    dynamic_slice x0 -> x14, local copies, waits for them, and re-layouts: none -> 14 us  [on_device(): lax.dynamic_slice(source, (own_index ^ partner, c, 0, 0), (1, 1, dev_rows...]
  transfers between devices with their start and end apart: 2 -> 42, of which waited for: 1 -> 17; matrix products, arithmetic and copies ran while one was open for 4% -> 9% of each run, Pallas kernels for 0% -> 32%
where the time goes in v2:
time: 282 us; the launch traced here: 277 us
  Pallas kernels  91.7 us (33%)
  waiting for transfers between devices  81.5 us (29%)
  starting transfers between devices  71.5 us (25%)
  local copies, waits for them, and re-layouts  15.2 us (5%)
  other arithmetic  14.2 us (5%)
    pallas_call x2, Pallas kernels, block_call(): pl.pallas_call(functools.partial(block_kernel, block, partners, whole), o...  86.9 us
    ppermute x21, waiting for transfers between devices, swap(): return lax.ppermute(piece, 'dp', [(i, i ^ partner) for i in range(size)])  46 us
    ppermute x21, starting transfers between devices, swap(): return lax.ppermute(piece, 'dp', [(i, i ^ partner) for i in range(size)])  38.7 us
    ppermute x20, waiting for transfers between devices, sum_over(): lax.ppermute(value, axis, [(i, (i + shift) % size) for i in range(size)])  35.5 us
    ppermute x20, starting transfers between devices, sum_over(): lax.ppermute(value, axis, [(i, (i + shift) % size) for i in range(size)])  28.5 us
    dynamic_slice x14, local copies, waits for them, and re-layouts, on_device(): lax.dynamic_slice(source, (own_index ^ partner, c, 0, 0), (1, 1, dev_rows...  14 us
    reduce_sum x1, other arithmetic, on_device(): graft_squares = jnp.sum(graft_step * graft_step)  7.33 us
  transfers between devices with their start and end apart: 42, of which 17 were waited for; matrix products, arithmetic and copies ran while one was open for 9% of the time, Pallas kernels for 32%

profile of v2, /device:TPU:12, one launch (start us, length us, event | category | flops | bytes accessed | tf_op | source)
XLA Modules:
  0.0 276.7 jit_solution(10510502149891053921)
XLA Ops:
  0.6 5.0 %fusion.5 = f32[]{:T(128)} fusion(bf16[4,4,128,1024]{3,2,1,0:T(8,128)(2,1)} %param.3), kind=kLoop, calls=%fused_computation.7 | loop fusion | flops 6291455 | bytes 4194308 | tf_op jit(solution)/shard_map/reduce_sum | solution.py:400
  23.9 3.5 %collective-permute-start.22 = (bf16[128,1024]{1,0:T(8,128)(2,1)S(1)}, bf16[128,1024]{1,0:T(8,128)(2,1)S(1)}, u32[]{:S(2)}, u32[]{:S(2)}) collective-permute-start(bf16[128,1024]{1,0:T(8,128)(2,1)S(1)} %bitcast.54), channel_id=1, source_target_pairs={{0,20},{4,16},{8,28},{12,24},{16,4},{20,0},{24,12},{28,8},{1,21},{... | collective-permute-start | bytes 786440 | tf_op jit(solution)/shard_map/ppermute | solution.py:375
  31.5 17.3 %collective-permute-done.3 = f32[1,128]{1,0:T(1,128)S(1)} collective-permute-done((f32[1,128]{1,0:T(1,128)S(1)}, f32[1,128]{1,0:T(1,128)S(1)}, u32[]{:S(2)}, u32[]{:S(2)}) %collective-permute-start.3) | collective-permute-done | bytes 544 | tf_op jit(solution)/shard_map/ppermute | solution.py:381
  49.2 3.1 %collective-permute-done.4 = f32[1,128]{1,0:T(1,128)S(1)} collective-permute-done((f32[1,128]{1,0:T(1,128)S(1)}, f32[1,128]{1,0:T(1,128)S(1)}, u32[]{:S(2)}, u32[]{:S(2)}) %collective-permute-start.4) | collective-permute-done | bytes 544 | tf_op jit(solution)/shard_map/ppermute | solution.py:381
  52.3 2.8 %collective-permute-start.5 = (f32[1,128]{1,0:T(1,128)S(1)}, f32[1,128]{1,0:T(1,128)S(1)}, u32[]{:S(2)}, u32[]{:S(2)}) collective-permute-start(f32[1,128]{1,0:T(1,128)S(1)} %add_add_fusion.3), channel_id=1, source_target_pairs={{0,12},{4,16},{8,20},{12,24},{16,28},{20,0},{24,4},{28,8},{1,13},{... | collective-permute-start | bytes 1544 | tf_op jit(solution)/shard_map/ppermute | solution.py:381
  58.7 2.6 collective-permute-done.6
  61.3 2.8 %collective-permute-start.7 = (f32[1,128]{1,0:T(1,128)S(1)}, f32[1,128]{1,0:T(1,128)S(1)}, u32[]{:S(2)}, u32[]{:S(2)}) collective-permute-start(f32[1,128]{1,0:T(1,128)S(1)} %add_add_fusion.3), channel_id=1, source_target_pairs={{0,20},{4,24},{8,28},{12,0},{16,4},{20,8},{24,12},{28,16},{1,21},{... | collective-permute-start | bytes 1544 | tf_op jit(solution)/shard_map/ppermute | solution.py:381
  64.1 2.6 collective-permute-done.7
  72.1 4.9 %collective-permute-done.9 = f32[1,128]{1,0:T(1,128)S(1)} collective-permute-done((f32[1,128]{1,0:T(1,128)S(1)}, f32[1,128]{1,0:T(1,128)S(1)}, u32[]{:S(2)}, u32[]{:S(2)}) %collective-permute-start.9) | collective-permute-done | bytes 544 | tf_op jit(solution)/shard_map/ppermute | solution.py:381
  77.0 3.3 %collective-permute-start.14 = (bf16[128,1024]{1,0:T(8,128)(2,1)S(1)}, bf16[128,1024]{1,0:T(8,128)(2,1)}, u32[]{:S(2)}, u32[]{:S(2)}) collective-permute-start(bf16[128,1024]{1,0:T(8,128)(2,1)S(1)} %bitcast.51), channel_id=1, source_target_pairs={{0,16},{4,20},{8,24},{12,28},{16,0},{20,4},{24,8},{28,12},{1,17},{... | collective-permute-start | bytes 786440 | tf_op jit(solution)/shard_map/ppermute | solution.py:375
  85.5 7.3 %fusion.4 = (f32[]{:T(128)}, f32[4,4,128,1024]{3,2,1,0:T(8,128)}) fusion(bf16[4,4,128,1024]{3,2,1,0:T(8,128)(2,1)S(1)} %copy-done.1, f32[]{:T(128)} %bitcast.1, f32[4,4,128,1024]{3,2,1,0:T(8,128)} %param.5), kind=kLoop, calls=%fused_computation.6 | loop fusion | flops 14680063 | bytes 20971528 | tf_op jit(solution)/shard_map/reduce_sum | solution.py:423
  92.9 3.0 %collective-permute-done.14.rest_4_ = bf16[128,1024]{1,0:T(8,128)(2,1)} collective-permute-done((bf16[128,1024]{1,0:T(8,128)(2,1)S(1)}, bf16[128,1024]{1,0:T(8,128)(2,1)}, u32[]{:S(2)}, u32[]{:S(2)}) %collective-permute-start.14) | collective-permute-done | bytes 262176 | tf_op jit(solution)/shard_map/ppermute | solution.py:375
  95.9 4.0 %collective-permute-start.21 = (bf16[128,1024]{1,0:T(8,128)(2,1)S(1)}, bf16[128,1024]{1,0:T(8,128)(2,1)}, u32[]{:S(2)}, u32[]{:S(2)}) collective-permute-start(bf16[128,1024]{1,0:T(8,128)(2,1)S(1)} %bitcast.48), channel_id=1, source_target_pairs={{0,16},{4,20},{8,24},{12,28},{16,0},{20,4},{24,8},{28,12},{1,17},{... | collective-permute-start | bytes 786440 | tf_op jit(solution)/shard_map/ppermute | solution.py:375
  99.8 9.1 %collective-permute-done.13.rest_3_ = bf16[128,1024]{1,0:T(8,128)(2,1)} collective-permute-done((bf16[128,1024]{1,0:T(8,128)(2,1)S(1)}, bf16[128,1024]{1,0:T(8,128)(2,1)}, u32[]{:S(2)}, u32[]{:S(2)}) %collective-permute-start.13) | collective-permute-done | bytes 262176 | tf_op jit(solution)/shard_map/ppermute | solution.py:375
  108.9 4.0 %collective-permute-start.20 = (bf16[128,1024]{1,0:T(8,128)(2,1)S(1)}, bf16[128,1024]{1,0:T(8,128)(2,1)}, u32[]{:S(2)}, u32[]{:S(2)}) collective-permute-start(bf16[128,1024]{1,0:T(8,128)(2,1)S(1)} %bitcast.46), channel_id=1, source_target_pairs={{0,28},{4,24},{8,20},{12,16},{16,12},{20,8},{24,4},{28,0},{1,29},{... | collective-permute-start | bytes 786440 | tf_op jit(solution)/shard_map/ppermute | solution.py:375
  114.9 8.3 %collective-permute-done.10.rest_0_ = bf16[128,1024]{1,0:T(8,128)(2,1)S(1)} collective-permute-done((bf16[128,1024]{1,0:T(8,128)(2,1)S(1)}, bf16[128,1024]{1,0:T(8,128)(2,1)S(1)}, u32[]{:S(2)}, u32[]{:S(2)}) %collective-permute-start.10) | collective-permute-done | bytes 262176 | tf_op jit(solution)/shard_map/ppermute | solution.py:375
  125.7 43.6 %shard_map.58 = (f32[4,1024,1024]{2,1,0:T(8,128)}, bf16[1024,1024]{1,0:T(8,128)(2,1)}, f32[1,128]{1,0:T(1,128)}) custom-call(s32[1]{0:T(128)} %bitcast.me_ref, f32[1]{0:T(128)} %bitcast.2.scale_ref, bf16[8,2,128,1024]{3,2,1,0:T(8,128)(2,1)} %bitcast.38, f32[4,1024,1024]{2,1,0:T(8,128)} %bitcast.57, bf16[128,1024]{1,0:T(8,128)(2,1)} %copy-done.9, ...), custom_call_target="tpu_custom_call" | custom-call | flops 34359738368 | bytes 20971520 | tf_op jit(solution)/shard_map/pallas_call | solution.py:261
  169.2 4.3 %all-to-all-start = ((bf16[8,128,1024]{2,1,0:T(8,128)(2,1)}), bf16[8,128,1024]{2,1,0:T(8,128)(2,1)S(1)}, u32[]{:S(2)}, u32[]{:S(2)}) async-start(bf16[8,128,1024]{2,1,0:T(8,128)(2,1)} %bitcast.41), calls=%async_computation | async-start | bytes 4194304 | tf_op jit(solution)/shard_map/all_to_all | solution.py:390
  173.6 43.3 %shard_map.59 = (f32[4,1024,1024]{2,1,0:T(8,128)}, bf16[128,1024]{1,0:T(8,128)(2,1)}, bf16[128,1024]{1,0:T(8,128)(2,1)}, bf16[128,1024]{1,0:T(8,128)(2,1)}, bf16...) custom-call(s32[1]{0:T(128)} %bitcast.me_ref, ...), custom_call_target="tpu_custom_call", output_to_operand_aliasing={{0}: (11, {})} | custom-call | flops 34359738368 | bytes 20971520 | tf_op jit(solution)/shard_map/pallas_call | solution.py:261
  226.4 3.6 %collective-permute-start.29 = (f32[1,128]{1,0:T(1,128)S(1)}, f32[1,128]{1,0:T(1,128)S(1)}, u32[]{:S(2)}, u32[]{:S(2)}) collective-permute-start(f32[1,128]{1,0:T(1,128)S(1)} %add_add_fusion.1), channel_id=1, source_target_pairs={{0,12},{4,16},{8,20},{12,24},{16,28},{20,0},{24,4},{28,8},{1,13},{... | collective-permute-start | bytes 1544 | tf_op jit(solution)/shard_map/ppermute | solution.py:381
  230.6 2.9 %collective-permute-start.31 = (f32[1,128]{1,0:T(1,128)S(1)}, f32[1,128]{1,0:T(1,128)S(1)}, u32[]{:S(2)}, u32[]{:S(2)}) collective-permute-start(f32[1,128]{1,0:T(1,128)S(1)} %add_add_fusion.1), channel_id=1, source_target_pairs={{0,20},{4,24},{8,28},{12,0},{16,4},{20,8},{24,12},{28,16},{1,21},{... | collective-permute-start | bytes 1544 | tf_op jit(solution)/shard_map/ppermute | solution.py:381
  248.6 16.8 %collective-permute-done.37.rest_4_ = bf16[128,1024]{1,0:T(8,128)(2,1)S(1)} collective-permute-done((bf16[128,1024]{1,0:T(8,128)(2,1)}, bf16[128,1024]{1,0:T(8,128)(2,1)S(1)}, u32[]{:S(2)}, u32[]{:S(2)}) %collective-permute-start.37) | collective-permute-done | bytes 262176 | tf_op jit(solution)/shard_map/ppermute | solution.py:375
  265.4 4.9 %collective-permute-done.38.rest_5_ = bf16[128,1024]{1,0:T(8,128)(2,1)S(1)} collective-permute-done((bf16[128,1024]{1,0:T(8,128)(2,1)}, bf16[128,1024]{1,0:T(8,128)(2,1)S(1)}, u32[]{:S(2)}, u32[]{:S(2)}) %collective-permute-start.38) | collective-permute-done | bytes 262176 | tf_op jit(solution)/shard_map/ppermute | solution.py:375
  270.3 3.9 %collective-permute-done.39.rest_6_ = bf16[128,1024]{1,0:T(8,128)(2,1)} collective-permute-done((bf16[128,1024]{1,0:T(8,128)(2,1)}, bf16[128,1024]{1,0:T(8,128)(2,1)}, u32[]{:S(2)}, u32[]{:S(2)}) %collective-permute-start.39) | collective-permute-done | bytes 262176 | tf_op jit(solution)/shard_map/ppermute | solution.py:375
  (107 shorter events, 67.3 us)
Async XLA Ops:
  6.2 21.2 %collective-permute-start = (f32[1,128]{1,0:T(1,128)S(1)}, f32[1,128]{1,0:T(1,128)S(1)}, u32[]{:S(2)}, u32[]{:S(2)}) collective-permute-start(f32[1,128]{1,0:T(1,128)S(1)} %broadcast_in_dim.10), channel_id=1, source_target_pairs={{0,1},{1,2},{2,3},{3,0},{4,5},{5,6},{6,7},{7,4},{8,9},{9,10},{10,1... | collective-permute-start | bytes 1544 | tf_op jit(solution)/shard_map/ppermute | solution.py:381
  6.3 21.6 %collective-permute-start.1 = (f32[1,128]{1,0:T(1,128)S(1)}, f32[1,128]{1,0:T(1,128)S(1)}, u32[]{:S(2)}, u32[]{:S(2)}) collective-permute-start(f32[1,128]{1,0:T(1,128)S(1)} %broadcast_in_dim.10), channel_id=1, source_target_pairs={{0,2},{1,3},{2,0},{3,1},{4,6},{5,7},{6,4},{7,5},{8,10},{9,11},{10,... | collective-permute-start | bytes 1544 | tf_op jit(solution)/shard_map/ppermute | solution.py:381
  7.9 21.4 %collective-permute-start.2 = (f32[1,128]{1,0:T(1,128)S(1)}, f32[1,128]{1,0:T(1,128)S(1)}, u32[]{:S(2)}, u32[]{:S(2)}) collective-permute-start(f32[1,128]{1,0:T(1,128)S(1)} %broadcast_in_dim.10), channel_id=1, source_target_pairs={{0,3},{1,0},{2,1},{3,2},{4,7},{5,4},{6,5},{7,6},{8,11},{9,8},{10,9... | collective-permute-start | bytes 1544 | tf_op jit(solution)/shard_map/ppermute | solution.py:381
  23.3 57.2 %collective-permute-start.23 = (bf16[128,1024]{1,0:T(8,128)(2,1)S(1)}, bf16[128,1024]{1,0:T(8,128)(2,1)S(1)}, u32[]{:S(2)}, u32[]{:S(2)}) collective-permute-start(bf16[128,1024]{1,0:T(8,128)(2,1)S(1)} %bitcast.55), channel_id=1, source_target_pairs={{0,4},{4,0},{8,12},{12,8},{16,20},{20,16},{24,28},{28,24},{1,5},{5... | collective-permute-start | bytes 786440 | tf_op jit(solution)/shard_map/ppermute | solution.py:375
  23.9 56.7 %collective-permute-start.22 = (bf16[128,1024]{1,0:T(8,128)(2,1)S(1)}, bf16[128,1024]{1,0:T(8,128)(2,1)S(1)}, u32[]{:S(2)}, u32[]{:S(2)}) collective-permute-start(bf16[128,1024]{1,0:T(8,128)(2,1)S(1)} %bitcast.54), channel_id=1, source_target_pairs={{0,20},{4,16},{8,28},{12,24},{16,4},{20,0},{24,12},{28,8},{1,21},{... | collective-permute-start | bytes 786440 | tf_op jit(solution)/shard_map/ppermute | solution.py:375
  27.4 55.5 %collective-permute-start.16 = (bf16[128,1024]{1,0:T(8,128)(2,1)S(1)}, bf16[128,1024]{1,0:T(8,128)(2,1)S(1)}, u32[]{:S(2)}, u32[]{:S(2)}) collective-permute-start(bf16[128,1024]{1,0:T(8,128)(2,1)S(1)} %bitcast.53), channel_id=1, source_target_pairs={{0,4},{4,0},{8,12},{12,8},{16,20},{20,16},{24,28},{28,24},{1,5},{5... | collective-permute-start | bytes 786440 | tf_op jit(solution)/shard_map/ppermute | solution.py:375
  27.9 55.0 %collective-permute-start.15 = (bf16[128,1024]{1,0:T(8,128)(2,1)S(1)}, bf16[128,1024]{1,0:T(8,128)(2,1)S(1)}, u32[]{:S(2)}, u32[]{:S(2)}) collective-permute-start(bf16[128,1024]{1,0:T(8,128)(2,1)S(1)} %bitcast.52), channel_id=1, source_target_pairs={{0,20},{4,16},{8,28},{12,24},{16,4},{20,0},{24,12},{28,8},{1,21},{... | collective-permute-start | bytes 786440 | tf_op jit(solution)/shard_map/ppermute | solution.py:375
  29.9 18.9 %collective-permute-start.3 = (f32[1,128]{1,0:T(1,128)S(1)}, f32[1,128]{1,0:T(1,128)S(1)}, u32[]{:S(2)}, u32[]{:S(2)}) collective-permute-start(f32[1,128]{1,0:T(1,128)S(1)} %add_add_fusion.3), channel_id=1, source_target_pairs={{0,4},{4,8},{8,12},{12,16},{16,20},{20,24},{24,28},{28,0},{1,5},{5... | collective-permute-start | bytes 1544 | tf_op jit(solution)/shard_map/ppermute | solution.py:381
  80.5 28.5 %collective-permute-start.13 = (bf16[128,1024]{1,0:T(8,128)(2,1)S(1)}, bf16[128,1024]{1,0:T(8,128)(2,1)}, u32[]{:S(2)}, u32[]{:S(2)}) collective-permute-start(bf16[128,1024]{1,0:T(8,128)(2,1)S(1)} %bitcast.50), channel_id=1, source_target_pairs={{0,28},{4,24},{8,20},{12,16},{16,12},{20,8},{24,4},{28,0},{1,29},{... | collective-permute-start | bytes 786440 | tf_op jit(solution)/shard_map/ppermute | solution.py:375
  80.6 32.3 %collective-permute-start.12 = (bf16[128,1024]{1,0:T(8,128)(2,1)S(1)}, bf16[128,1024]{1,0:T(8,128)(2,1)S(1)}, u32[]{:S(2)}, u32[]{:S(2)}) collective-permute-start(bf16[128,1024]{1,0:T(8,128)(2,1)S(1)} %bitcast.49), channel_id=1, source_target_pairs={{0,12},{4,8},{8,4},{12,0},{16,28},{20,24},{24,20},{28,16},{1,13},{... | collective-permute-start | bytes 786440 | tf_op jit(solution)/shard_map/ppermute | solution.py:375
  82.9 30.0 %collective-permute-start.11 = (bf16[128,1024]{1,0:T(8,128)(2,1)S(1)}, bf16[128,1024]{1,0:T(8,128)(2,1)S(1)}, u32[]{:S(2)}, u32[]{:S(2)}) collective-permute-start(bf16[128,1024]{1,0:T(8,128)(2,1)S(1)} %bitcast.47), channel_id=1, source_target_pairs={{0,8},{4,12},{8,0},{12,4},{16,24},{20,28},{24,16},{28,20},{1,9},{5... | collective-permute-start | bytes 786440 | tf_op jit(solution)/shard_map/ppermute | solution.py:375
  83.0 40.2 %collective-permute-start.10 = (bf16[128,1024]{1,0:T(8,128)(2,1)S(1)}, bf16[128,1024]{1,0:T(8,128)(2,1)S(1)}, u32[]{:S(2)}, u32[]{:S(2)}) collective-permute-start(bf16[128,1024]{1,0:T(8,128)(2,1)S(1)} %bitcast.44), channel_id=1, source_target_pairs={{0,24},{4,28},{8,16},{12,20},{16,8},{20,12},{24,0},{28,4},{1,25},{... | collective-permute-start | bytes 786440 | tf_op jit(solution)/shard_map/ppermute | solution.py:375
  95.9 77.7 %collective-permute-start.21 = (bf16[128,1024]{1,0:T(8,128)(2,1)S(1)}, bf16[128,1024]{1,0:T(8,128)(2,1)}, u32[]{:S(2)}, u32[]{:S(2)}) collective-permute-start(bf16[128,1024]{1,0:T(8,128)(2,1)S(1)} %bitcast.48), channel_id=1, source_target_pairs={{0,16},{4,20},{8,24},{12,28},{16,0},{20,4},{24,8},{28,12},{1,17},{... | collective-permute-start | bytes 786440 | tf_op jit(solution)/shard_map/ppermute | solution.py:375
  108.9 64.6 %collective-permute-start.20 = (bf16[128,1024]{1,0:T(8,128)(2,1)S(1)}, bf16[128,1024]{1,0:T(8,128)(2,1)}, u32[]{:S(2)}, u32[]{:S(2)}) collective-permute-start(bf16[128,1024]{1,0:T(8,128)(2,1)S(1)} %bitcast.46), channel_id=1, source_target_pairs={{0,28},{4,24},{8,20},{12,16},{16,12},{20,8},{24,4},{28,0},{1,29},{... | collective-permute-start | bytes 786440 | tf_op jit(solution)/shard_map/ppermute | solution.py:375
  112.9 60.7 %collective-permute-start.19 = (bf16[128,1024]{1,0:T(8,128)(2,1)S(1)}, bf16[128,1024]{1,0:T(8,128)(2,1)}, u32[]{:S(2)}, u32[]{:S(2)}) collective-permute-start(bf16[128,1024]{1,0:T(8,128)(2,1)S(1)} %bitcast.45), channel_id=1, source_target_pairs={{0,12},{4,8},{8,4},{12,0},{16,28},{20,24},{24,20},{28,16},{1,13},{... | collective-permute-start | bytes 786440 | tf_op jit(solution)/shard_map/ppermute | solution.py:375
  113.0 60.6 %collective-permute-start.18 = (bf16[128,1024]{1,0:T(8,128)(2,1)S(1)}, bf16[128,1024]{1,0:T(8,128)(2,1)}, u32[]{:S(2)}, u32[]{:S(2)}) collective-permute-start(bf16[128,1024]{1,0:T(8,128)(2,1)S(1)} %bitcast.43), channel_id=1, source_target_pairs={{0,8},{4,12},{8,0},{12,4},{16,24},{20,28},{24,16},{28,20},{1,9},{5... | collective-permute-start | bytes 786440 | tf_op jit(solution)/shard_map/ppermute | solution.py:375
  123.2 50.4 %collective-permute-start.17 = (bf16[128,1024]{1,0:T(8,128)(2,1)S(1)}, bf16[128,1024]{1,0:T(8,128)(2,1)}, u32[]{:S(2)}, u32[]{:S(2)}) collective-permute-start(bf16[128,1024]{1,0:T(8,128)(2,1)S(1)} %bitcast.42), channel_id=1, source_target_pairs={{0,24},{4,28},{8,16},{12,20},{16,8},{20,12},{24,0},{28,4},{1,25},{... | collective-permute-start | bytes 786440 | tf_op jit(solution)/shard_map/ppermute | solution.py:375
  169.2 76.9 %all-to-all-start = ((bf16[8,128,1024]{2,1,0:T(8,128)(2,1)}), bf16[8,128,1024]{2,1,0:T(8,128)(2,1)S(1)}, u32[]{:S(2)}, u32[]{:S(2)}) async-start(bf16[8,128,1024]{2,1,0:T(8,128)(2,1)} %bitcast.41), calls=%async_computation | async-start | bytes 4194304 | tf_op jit(solution)/shard_map/all_to_all | solution.py:390
  217.0 24.8 %collective-permute-start.34 = (bf16[128,1024]{1,0:T(8,128)(2,1)}, bf16[128,1024]{1,0:T(8,128)(2,1)S(1)}, u32[]{:S(2)}, u32[]{:S(2)}) collective-permute-start(bf16[128,1024]{1,0:T(8,128)(2,1)} %get-tuple-element.74), channel_id=1, source_target_pairs={{0,24},{4,28},{8,16},{12,20},{16,8},{20,12},{24,0},{28,4},{1,25},{... | collective-permute-start | bytes 786440 | tf_op jit(solution)/shard_map/ppermute | solution.py:375
  218.5 25.8 %collective-permute-start.35 = (bf16[128,1024]{1,0:T(8,128)(2,1)}, bf16[128,1024]{1,0:T(8,128)(2,1)S(1)}, u32[]{:S(2)}, u32[]{:S(2)}) collective-permute-start(bf16[128,1024]{1,0:T(8,128)(2,1)} %get-tuple-element.75), channel_id=1, source_target_pairs={{0,8},{4,12},{8,0},{12,4},{16,24},{20,28},{24,16},{28,20},{1,9},{5... | collective-permute-start | bytes 786440 | tf_op jit(solution)/shard_map/ppermute | solution.py:375
  238.0 27.4 %collective-permute-start.37 = (bf16[128,1024]{1,0:T(8,128)(2,1)}, bf16[128,1024]{1,0:T(8,128)(2,1)S(1)}, u32[]{:S(2)}, u32[]{:S(2)}) collective-permute-start(bf16[128,1024]{1,0:T(8,128)(2,1)} %get-tuple-element.77), channel_id=1, source_target_pairs={{0,28},{4,24},{8,20},{12,16},{16,12},{20,8},{24,4},{28,0},{1,29},{... | collective-permute-start | bytes 786440 | tf_op jit(solution)/shard_map/ppermute | solution.py:375
  239.8 30.5 %collective-permute-start.38 = (bf16[128,1024]{1,0:T(8,128)(2,1)}, bf16[128,1024]{1,0:T(8,128)(2,1)S(1)}, u32[]{:S(2)}, u32[]{:S(2)}) collective-permute-start(bf16[128,1024]{1,0:T(8,128)(2,1)} %get-tuple-element.78), channel_id=1, source_target_pairs={{0,16},{4,20},{8,24},{12,28},{16,0},{20,4},{24,8},{28,12},{1,17},{... | collective-permute-start | bytes 786440 | tf_op jit(solution)/shard_map/ppermute | solution.py:375
  241.8 32.4 %collective-permute-start.39 = (bf16[128,1024]{1,0:T(8,128)(2,1)}, bf16[128,1024]{1,0:T(8,128)(2,1)}, u32[]{:S(2)}, u32[]{:S(2)}) collective-permute-start(bf16[128,1024]{1,0:T(8,128)(2,1)} %get-tuple-element.79), channel_id=1, source_target_pairs={{0,20},{4,16},{8,28},{12,24},{16,4},{20,0},{24,12},{28,8},{1,21},{... | collective-permute-start | bytes 786440 | tf_op jit(solution)/shard_map/ppermute | solution.py:375
  244.3 29.9 %collective-permute-start.40 = (bf16[128,1024]{1,0:T(8,128)(2,1)}, bf16[128,1024]{1,0:T(8,128)(2,1)}, u32[]{:S(2)}, u32[]{:S(2)}) collective-permute-start(bf16[128,1024]{1,0:T(8,128)(2,1)} %get-tuple-element.80), channel_id=1, source_target_pairs={{0,4},{4,0},{8,12},{12,8},{16,20},{20,16},{24,28},{28,24},{1,5},{5... | collective-permute-start | bytes 786440 | tf_op jit(solution)/shard_map/ppermute | solution.py:375
  (28 other events, 292.8 us)

commit v3 on v2

--- a/solution.py
+++ b/solution.py
@@ -157,8 +157,12 @@
         grad_in.append(pltpu.make_async_copy(received[n], grads.at[0, rows_of(partner), :], sem_g.at[n + 1]))
     for copy in grad_in:
         copy.start()
-    stat_in = pltpu.make_async_copy(stat_hbm.at[pl.ds(2 * block, 2)], stat_old, sem_s)
-    stat_in.start()
+
+    def stat_load(s):
+        return pltpu.make_async_copy(stat_hbm.at[2 * block + s], stat_old.at[s], sem_s.at[s])
+
+    for s in range(2):
+        stat_load(s).start()
     for copy in grad_in:
         copy.wait()
     scale = scale_ref[0]
@@ -167,9 +171,9 @@
     bias = jnp.where(eye, 1.25, 0.0)
     for start, stop in panels(width):
         grads[1, :, start:stop] = grads[0, start:stop, :].T
-    stat_in.wait()
 
     def gram_step(s, carry):
+        stat_load(s).wait()
         total = jnp.zeros((8, PANEL), jnp.float32)
         for start, stop in panels(width):
             gram = scale * dot_f32(grads[s, :stop, :], grads[1 - s, :, start:stop])
@@ -189,19 +193,24 @@
     stat_done.start()
 
     def root_step(s, carry):
-        left_root[...] = root[...]
         z = 2.5 / jnp.sqrt(jnp.sum(sums[s], keepdims=True) + 1e-06)
-        root0 = jnp.sqrt(jnp.sqrt(z)).astype(jnp.bfloat16).astype(jnp.float32)
-        for start, stop in panels(width):
-            for low, high in panels(width):
-                scaled = z * stat[s, low:high, start:stop]
-                first = -0.25 * scaled
-                if low == start:
-                    first = bias + first
-                first = first.astype(jnp.bfloat16)
-                matrix[low:high, start:stop] = scaled.astype(jnp.bfloat16)
-                factor[low:high, start:stop] = first
-                root[low:high, start:stop] = (root0 * first.astype(jnp.float32)).astype(jnp.bfloat16)
+        root0 = jnp.sqrt(jnp.sqrt(z)).astype(jnp.bfloat16)
+
+        def begin(row, cols, offset):
+            scaled = z * stat[s, row, cols]
+            first = (offset - 0.25 * scaled).astype(jnp.bfloat16)
+            matrix[row, cols] = scaled.astype(jnp.bfloat16)
+            factor[row, cols] = first
+            root[row, cols] = root0 * first
+
+        def begin_panel(n, inner):
+            row = pl.ds(pl.multiple_of(n * PANEL, PANEL), PANEL)
+            for start, stop in panels(width):
+                begin(row, slice(start, stop), 0.0)
+            begin(row, row, bias)
+            return inner
+
+        lax.fori_loop(0, width // PANEL, begin_panel, 0)
 
         def next_factor(value, start, stop):
             factor[start:stop, start:stop] = (bias - 0.25 * value[start:]).astype(jnp.bfloat16)
@@ -218,6 +227,11 @@
             return inner
 
         lax.fori_loop(0, ITERS - 1, newton, 0)
+
+        @pl.when(s == 0)
+        def _():
+            left_root[...] = root[...]
+
         return carry
 
     lax.fori_loop(0, 2, root_step, 0)
@@ -274,7 +288,7 @@
             *[pltpu.VMEM(square, jnp.bfloat16) for _ in range(6)],
             pltpu.VMEM((2, 8, PANEL), jnp.float32),
             pltpu.SemaphoreType.DMA((len(partners) + 1,)),
-            pltpu.SemaphoreType.DMA,
+            pltpu.SemaphoreType.DMA((2,)),
             pltpu.SemaphoreType.DMA,
             pltpu.SemaphoreType.DMA((len(partners) + 1,)),
         ],
@@ -285,78 +299,108 @@
     return results[0], results[1:-1], results[-1]
 
 
-def scale_rows(ratio_ref, rows_ref, *rest):
-    out_ref = rest[-1]
-    out_ref[...] = ratio_ref[0] * rows_ref[...].astype(jnp.float32)
-
-
-def scale_whole(chunk, chunks, ratio, rows, carried):
-    owners, dev_rows, width = rows.shape
-    step = max(1, owners // 4)
-    operands = [ratio, rows]
-    in_specs = [
-        pl.BlockSpec(memory_space=pltpu.SMEM),
-        pl.BlockSpec((step, dev_rows, width), lambda i: (i, 0, 0)),
+def gather_kernel(chunk, partners, me_ref, grad_hbm, *rest):
+    count = len(partners)
+    outs = rest[:count]
+    squares_out, held, sem_in, sem_out = rest[count:]
+    me = me_ref[0]
+    loads = [
+        pltpu.make_async_copy(grad_hbm.at[me ^ partner, chunk], held.at[n], sem_in.at[n])
+        for n, partner in enumerate((*partners, 0))
     ]
-    aliases = {}
-    if carried is not None:
-        aliases = {len(operands): 0}
-        operands.append(carried)
-        in_specs.append(pl.BlockSpec(memory_space=pltpu.HBM))
-    return pl.pallas_call(
-        scale_rows,
-        grid=(owners // step,),
-        out_shape=jax.ShapeDtypeStruct((owners, chunks, dev_rows, width), jnp.float32),
-        in_specs=in_specs,
-        out_specs=pl.BlockSpec((step, None, dev_rows, width), lambda i: (i, chunk, 0, 0)),
-        input_output_aliases=aliases,
-        compiler_params=pltpu.CompilerParams(vmem_limit_bytes=16 * 1024 * 1024),
-        cost_estimate=pl.CostEstimate(flops=rows.size, bytes_accessed=6 * rows.size, transcendentals=0),
-    )(*operands)
-
-
-def scale_kernel(chunk, partners, me_ref, ratio_ref, *rest):
-    count = len(partners) + 1
-    pieces = rest[:count]
-    out_ref, narrow, wide, sem_in, sem_out = rest[-5:]
-    me = me_ref[0]
-    loads = [pltpu.make_async_copy(pieces[n], narrow.at[n], sem_in.at[n]) for n in range(count)]
     for load in loads:
         load.start()
     stores = []
-    for n, partner in enumerate((0, *partners)):
+    for n in range(count):
+        loads[n].wait()
+        store = pltpu.make_async_copy(held.at[n], outs[n], sem_out.at[n])
+        store.start()
+        stores.append(store)
+    loads[count].wait()
+    rows = 16
+
+    def add_rows(i, total):
+        at = pl.multiple_of(i * rows, rows)
+        for n in range(count + 1):
+            wide = held[n, pl.ds(at, rows), :].astype(jnp.float32)
+            total = total + wide * wide
+        return total
+
+    width = held.shape[2]
+    total = lax.fori_loop(0, held.shape[1] // rows, add_rows, jnp.zeros((rows, width), jnp.float32))
+    squares_out[...] = jnp.broadcast_to(jnp.sum(total, keepdims=True), squares_out.shape)
+    for store in stores:
+        store.wait()
+
+
+def gather_call(chunk, partners, me, by_owner):
+    dev_rows, width = by_owner.shape[2:]
+    hbm = pl.BlockSpec(memory_space=pltpu.HBM)
+    count = len(partners)
+    size = (count + 1) * dev_rows * width
+    results = pl.pallas_call(
+        functools.partial(gather_kernel, chunk, partners),
+        out_shape=(
+            *[jax.ShapeDtypeStruct((dev_rows, width), jnp.bfloat16) for _ in partners],
+            jax.ShapeDtypeStruct((1, 128), jnp.float32),
+        ),
+        in_specs=[pl.BlockSpec(memory_space=pltpu.SMEM), hbm],
+        out_specs=(*[hbm] * count, pl.BlockSpec(memory_space=pltpu.VMEM)),
+        scratch_shapes=[
+            pltpu.VMEM((count + 1, dev_rows, width), jnp.bfloat16),
+            pltpu.SemaphoreType.DMA((count + 1,)),
+            pltpu.SemaphoreType.DMA((count,)),
+        ],
+        compiler_params=pltpu.CompilerParams(vmem_limit_bytes=16 * 1024 * 1024),
+        cost_estimate=pl.CostEstimate(flops=2 * size, bytes_accessed=4 * size, transcendentals=0),
+    )(me, by_owner)
+    return results[:-1], results[-1]
+
+
+def scale_kernel(chunk, targets, me_ref, ratio_ref, *rest):
+    pieces = rest[: len(targets)]
+    out_ref, narrow, wide, sem_in, sem_out = rest[-5:]
+    me = me_ref[0]
+    if len(rest) < len(targets) + 5:
+        pieces = [rest[0].at[n] for n in range(len(targets))]
+    loads = [pltpu.make_async_copy(piece, narrow.at[n], sem_in.at[n]) for n, piece in enumerate(pieces)]
+    for load in loads:
+        load.start()
+    stores = []
+    for n, target in enumerate(targets):
         loads[n].wait()
         wide[n] = ratio_ref[0] * narrow[n].astype(jnp.float32)
-        store = pltpu.make_async_copy(wide.at[n], out_ref.at[me ^ partner, chunk], sem_out.at[n])
+        owner = n if target is None else me ^ target
+        store = pltpu.make_async_copy(wide.at[n], out_ref.at[owner, chunk], sem_out.at[n])
         store.start()
         stores.append(store)
     for store in stores:
         store.wait()
 
 
-def scale_pieces(chunk, chunks, partners, me, ratio, pieces, carried):
-    dev_rows, width = pieces[0].shape
-    owners = len(pieces)
+def scale_call(chunk, out_shape, targets, me, ratio, pieces, carried):
+    dev_rows, width = out_shape[2:]
+    count = len(targets)
     hbm = pl.BlockSpec(memory_space=pltpu.HBM)
     smem = pl.BlockSpec(memory_space=pltpu.SMEM)
     operands = [me, ratio, *pieces]
-    in_specs = [smem, smem] + [hbm] * owners
+    in_specs = [smem, smem] + [hbm] * len(pieces)
     aliases = {}
     if carried is not None:
         aliases = {len(operands): 0}
         operands.append(carried)
         in_specs.append(hbm)
-    size = owners * dev_rows * width
+    size = count * dev_rows * width
     return pl.pallas_call(
-        functools.partial(scale_kernel, chunk, partners),
-        out_shape=jax.ShapeDtypeStruct((owners, chunks, dev_rows, width), jnp.float32),
+        functools.partial(scale_kernel, chunk, targets),
+        out_shape=jax.ShapeDtypeStruct(out_shape, jnp.float32),
         in_specs=in_specs,
         out_specs=hbm,
         scratch_shapes=[
-            pltpu.VMEM((owners, dev_rows, width), jnp.bfloat16),
-            pltpu.VMEM((owners, dev_rows, width), jnp.float32),
-            pltpu.SemaphoreType.DMA((owners,)),
-            pltpu.SemaphoreType.DMA((owners,)),
+            pltpu.VMEM((count, dev_rows, width), jnp.bfloat16),
+            pltpu.VMEM((count, dev_rows, width), jnp.float32),
+            pltpu.SemaphoreType.DMA((count,)),
+            pltpu.SemaphoreType.DMA((count,)),
         ],
         input_output_aliases=aliases,
         compiler_params=pltpu.CompilerParams(vmem_limit_bytes=16 * 1024 * 1024),
@@ -366,7 +410,7 @@
 
 def partner_order(owners):
     half = owners // 2
-    order = (owners - 2, *range(2, half), owners - 1, *range(half, owners - 2), 1)
+    order = (owners - 2, owners - 1, *range(2, half), *range(half, owners - 2), 1)
     return tuple(dict.fromkeys(d for d in order if 0 < d < owners))
 
 
@@ -397,20 +441,16 @@
     chunks = statistics.shape[1] // 2
     by_owner = gradients.reshape(owners, chunks, dev_rows, block_width)
     grads_wide = gradients.astype(jnp.float32)
-    squares = jnp.full((1, 128), jnp.sum(grads_wide * grads_wide))
     partners = partner_order(owners)
-    own_index = lax.axis_index("dp")
-    me = own_index.astype(jnp.int32).reshape(1)
+    me = lax.axis_index("dp").astype(jnp.int32).reshape(1)
+    squares = jnp.zeros((1, 128), jnp.float32)
     received = []
-    source = by_owner
     for c in range(chunks):
+        pieces, part = gather_call(c, partners, me, by_owner)
+        squares = squares + part
         parts = []
-        for partner in partners:
-            piece = lax.dynamic_slice(
-                source, (own_index ^ partner, c, 0, 0), (1, 1, dev_rows, block_width)
-            )
-            source, piece = lax.optimization_barrier((source, piece))
-            parts.append(swap(piece.reshape(dev_rows, block_width), partner))
+        for partner, piece in zip(partners, pieces):
+            parts.append(swap(piece, partner))
         received.append(parts)
     grad_total = sum_over(squares, "mp")
     grad_total = sum_over(grad_total, "dp")[0, 0]
@@ -431,7 +471,7 @@
         )
         update_squares = update_squares + part
         if whole:
-            returned.append(exchange(product[0].reshape(owners, dev_rows, block_width)))
+            returned.append([exchange(product[0].reshape(owners, dev_rows, block_width))])
         else:
             parts = [product[0]]
             for n, partner in enumerate(partners):
@@ -443,11 +483,14 @@
     sums = sum_over(sums, "dp")
     graft_ratio = jnp.sqrt(sums[0, :1] / (sums[0, 1:2] + 1e-06))
     update = None
-    for c in range(chunks):
-        if c + 1 < chunks:
-            update = scale_whole(c, chunks, graft_ratio, returned[c], update)
-        else:
-            update = scale_pieces(c, chunks, partners, me, graft_ratio, returned[c], update)
+    out_shape = (owners, chunks, dev_rows, block_width)
+    for c in range(chunks - 1):
+        update = scale_call(c, out_shape, (None,) * owners, me, graft_ratio, returned[c], update)
+    late = partners[-2]
+    groups = (tuple(d for d in (0, *partners) if d != late), (late,))
+    for group in groups:
+        pieces = [dict(zip((0, *partners), returned[-1]))[d] for d in group]
+        update = scale_call(chunks - 1, out_shape, group, me, graft_ratio, pieces, update)
     return (update.reshape(gradients.shape), statistics_new[None], accumulated)
 
 

time: 282 us -> 272 us (0.965)
  waiting for transfers between devices: 81.5 us -> 99.4 us
  local copies, waits for them, and re-layouts: 15.2 us -> 2.8 us
  starting transfers between devices: 71.5 us -> 61.2 us
  other arithmetic: 14.2 us -> 8.76 us
    ppermute x20, waiting for transfers between devices: 35.5 us -> 60.1 us  [sum_over(): lax.ppermute(value, axis, [(i, (i + shift) % size) for i in range(size)])]
    ppermute x21, starting transfers between devices: 38.7 us -> 23.8 us  [swap(): return lax.ppermute(piece, 'dp', [(i, i ^ partner) for i in range(size)])]
    dynamic_slice x14 -> x0, local copies, waits for them, and re-layouts: 14 us -> none  [on_device(): lax.dynamic_slice(source, (own_index ^ partner, c, 0, 0), (1, 1, dev_rows...]
    ppermute x21, waiting for transfers between devices: 46 us -> 39.3 us  [swap(): return lax.ppermute(piece, 'dp', [(i, i ^ partner) for i in range(size)])]
    reduce_sum x1 -> x0, other arithmetic: 4.95 us -> none  [on_device(): squares = jnp.full((1, 128), jnp.sum(grads_wide * grads_wide))]
    ppermute x20, starting transfers between devices: 28.5 us -> 32.6 us  [sum_over(): lax.ppermute(value, axis, [(i, (i + shift) % size) for i in range(size)])]
    pallas_call x2 -> x5, Pallas kernels: 4.8 us -> 8.45 us  [the longest x3 6.43 us: scale_call(): pl.pallas_call(functools.partial(scale_kernel, chunk, targets), out_shape...]
    pallas_call x2, Pallas kernels: 86.9 us -> 83.8 us  [block_call(): pl.pallas_call(functools.partial(block_kernel, block, partners, whole), o...]
  transfers between devices with their start and end apart: 42 -> 42, of which waited for: 17 -> 21; matrix products, arithmetic and copies ran while one was open for 9% -> 4% of each run, Pallas kernels for 32% -> 33%
where the time goes in v3:
time: 272 us; the launch traced here: 267 us
  waiting for transfers between devices  99.4 us (37%)
  Pallas kernels  92.3 us (34%)
  starting transfers between devices  61.2 us (22%)
  other arithmetic  8.76 us (3%)
  local copies, waits for them, and re-layouts  2.8 us (1%)
    pallas_call x2, Pallas kernels, block_call(): pl.pallas_call(functools.partial(block_kernel, block, partners, whole), o...  83.8 us
    ppermute x20, waiting for transfers between devices, sum_over(): lax.ppermute(value, axis, [(i, (i + shift) % size) for i in range(size)])  60.1 us
    ppermute x21, waiting for transfers between devices, swap(): return lax.ppermute(piece, 'dp', [(i, i ^ partner) for i in range(size)])  39.3 us
    ppermute x20, starting transfers between devices, sum_over(): lax.ppermute(value, axis, [(i, (i + shift) % size) for i in range(size)])  32.6 us
    ppermute x21, starting transfers between devices, swap(): return lax.ppermute(piece, 'dp', [(i, i ^ partner) for i in range(size)])  23.8 us
    reduce_sum x1, other arithmetic, on_device(): graft_squares = jnp.sum(graft_step * graft_step)  7.38 us
    pallas_call x3, Pallas kernels, scale_call(): pl.pallas_call(functools.partial(scale_kernel, chunk, targets), out_shape...  6.43 us
  transfers between devices with their start and end apart: 42, of which 21 were waited for; matrix products, arithmetic and copies ran while one was open for 4% of the time, Pallas kernels for 33%

profile of v3, /device:TPU:12, one launch (start us, length us, event | category | flops | bytes accessed | tf_op | source)
XLA Modules:
  0.0 266.7 jit_solution(7172358096104280391)
XLA Ops:
  13.1 2.7 %collective-permute-start.3 = (f32[1,128]{1,0:T(1,128)S(1)}, f32[1,128]{1,0:T(1,128)S(1)}, u32[]{:S(2)}, u32[]{:S(2)}) collective-permute-start(f32[1,128]{1,0:T(1,128)S(1)} %add_add_fusion.3), channel_id=1, source_target_pairs={{0,4},{4,8},{8,12},{12,16},{16,20},{20,24},{24,28},{28,0},{1,5},{5... | collective-permute-start | bytes 1544 | tf_op jit(solution)/shard_map/ppermute | solution.py:425
  15.8 18.2 %collective-permute-done.3 = f32[1,128]{1,0:T(1,128)S(1)} collective-permute-done((f32[1,128]{1,0:T(1,128)S(1)}, f32[1,128]{1,0:T(1,128)S(1)}, u32[]{:S(2)}, u32[]{:S(2)}) %collective-permute-start.3) | collective-permute-done | bytes 544 | tf_op jit(solution)/shard_map/ppermute | solution.py:425
  34.7 3.8 %collective-permute-done.4 = f32[1,128]{1,0:T(1,128)S(1)} collective-permute-done((f32[1,128]{1,0:T(1,128)S(1)}, f32[1,128]{1,0:T(1,128)S(1)}, u32[]{:S(2)}, u32[]{:S(2)}) %collective-permute-start.4) | collective-permute-done | bytes 544 | tf_op jit(solution)/shard_map/ppermute | solution.py:425
  38.5 3.3 %collective-permute-start.5 = (f32[1,128]{1,0:T(1,128)S(1)}, f32[1,128]{1,0:T(1,128)S(1)}, u32[]{:S(2)}, u32[]{:S(2)}) collective-permute-start(f32[1,128]{1,0:T(1,128)S(1)} %add_add_fusion.3), channel_id=1, source_target_pairs={{0,12},{4,16},{8,20},{12,24},{16,28},{20,0},{24,4},{28,8},{1,13},{... | collective-permute-start | bytes 1544 | tf_op jit(solution)/shard_map/ppermute | solution.py:425
  41.8 3.3 %collective-permute-done.5 = f32[1,128]{1,0:T(1,128)S(1)} collective-permute-done((f32[1,128]{1,0:T(1,128)S(1)}, f32[1,128]{1,0:T(1,128)S(1)}, u32[]{:S(2)}, u32[]{:S(2)}) %collective-permute-start.5) | collective-permute-done | bytes 544 | tf_op jit(solution)/shard_map/ppermute | solution.py:425
  46.2 3.4 %collective-permute-done.6 = f32[1,128]{1,0:T(1,128)S(1)} collective-permute-done((f32[1,128]{1,0:T(1,128)S(1)}, f32[1,128]{1,0:T(1,128)S(1)}, u32[]{:S(2)}, u32[]{:S(2)}) %collective-permute-start.6) | collective-permute-done | bytes 544 | tf_op jit(solution)/shard_map/ppermute | solution.py:425
  49.5 3.8 %collective-permute-start.7 = (f32[1,128]{1,0:T(1,128)S(1)}, f32[1,128]{1,0:T(1,128)S(1)}, u32[]{:S(2)}, u32[]{:S(2)}) collective-permute-start(f32[1,128]{1,0:T(1,128)S(1)} %add_add_fusion.3), channel_id=1, source_target_pairs={{0,20},{4,24},{8,28},{12,0},{16,4},{20,8},{24,12},{28,16},{1,21},{... | collective-permute-start | bytes 1544 | tf_op jit(solution)/shard_map/ppermute | solution.py:425
  54.9 3.5 %collective-permute-start.8 = (f32[1,128]{1,0:T(1,128)S(1)}, f32[1,128]{1,0:T(1,128)S(1)}, u32[]{:S(2)}, u32[]{:S(2)}) collective-permute-start(f32[1,128]{1,0:T(1,128)S(1)} %add_add_fusion.3), channel_id=1, source_target_pairs={{0,24},{4,28},{8,0},{12,4},{16,8},{20,12},{24,16},{28,20},{1,25},{... | collective-permute-start | bytes 1544 | tf_op jit(solution)/shard_map/ppermute | solution.py:425
  60.4 14.1 %collective-permute-done.9 = f32[1,128]{1,0:T(1,128)S(1)} collective-permute-done((f32[1,128]{1,0:T(1,128)S(1)}, f32[1,128]{1,0:T(1,128)S(1)}, u32[]{:S(2)}, u32[]{:S(2)}) %collective-permute-start.9) | collective-permute-done | bytes 544 | tf_op jit(solution)/shard_map/ppermute | solution.py:425
  74.8 4.4 %collective-permute-start.16 = (bf16[128,1024]{1,0:T(8,128)(2,1)S(1)}, bf16[128,1024]{1,0:T(8,128)(2,1)}, u32[]{:S(2)}, u32[]{:S(2)}) collective-permute-start(bf16[128,1024]{1,0:T(8,128)(2,1)S(1)} %get-tuple-element.40), channel_id=1, source_target_pairs={{0,4},{4,0},{8,12},{12,8},{16,20},{20,16},{24,28},{28,24},{1,5},{5... | collective-permute-start | bytes 786440 | tf_op jit(solution)/shard_map/ppermute | solution.py:419
  80.7 7.4 %multiply_reduce_fusion = (f32[]{:T(128)}, f32[4,4,128,1024]{3,2,1,0:T(8,128)}) fusion(bf16[4,4,128,1024]{3,2,1,0:T(8,128)(2,1)S(1)} %copy-done.1, f32[]{:T(128)} %bitcast.2, f32[4,4,128,1024]{3,2,1,0:T(8,128)} %param.5), kind=kLoop, calls=%fused_computation | loop fusion | flops 14680063 | bytes 20971528 | tf_op jit(solution)/shard_map/reduce_sum | solution.py:463
  88.8 4.1 %collective-permute-done.15.rest_5_ = bf16[128,1024]{1,0:T(8,128)(2,1)} collective-permute-done((bf16[128,1024]{1,0:T(8,128)(2,1)S(1)}, bf16[128,1024]{1,0:T(8,128)(2,1)}, u32[]{:S(2)}, u32[]{:S(2)}) %collective-permute-start.15) | collective-permute-done | bytes 262176 | tf_op jit(solution)/shard_map/ppermute | solution.py:419
  92.9 3.2 %collective-permute-start.20 = (bf16[128,1024]{1,0:T(8,128)(2,1)S(1)}, bf16[128,1024]{1,0:T(8,128)(2,1)}, u32[]{:S(2)}, u32[]{:S(2)}) collective-permute-start(bf16[128,1024]{1,0:T(8,128)(2,1)S(1)} %get-tuple-element.45), channel_id=1, source_target_pairs={{0,12},{4,8},{8,4},{12,0},{16,28},{20,24},{24,20},{28,16},{1,13},{... | collective-permute-start | bytes 786440 | tf_op jit(solution)/shard_map/ppermute | solution.py:419
  96.1 3.2 %collective-permute-done.17.rest_0_ = bf16[128,1024]{1,0:T(8,128)(2,1)} collective-permute-done((bf16[128,1024]{1,0:T(8,128)(2,1)S(1)}, bf16[128,1024]{1,0:T(8,128)(2,1)}, u32[]{:S(2)}, u32[]{:S(2)}) %collective-permute-start.17) | collective-permute-done | bytes 262176 | tf_op jit(solution)/shard_map/ppermute | solution.py:419
  99.6 19.5 %collective-permute-done.18.rest_1_ = bf16[128,1024]{1,0:T(8,128)(2,1)} collective-permute-done((bf16[128,1024]{1,0:T(8,128)(2,1)S(1)}, bf16[128,1024]{1,0:T(8,128)(2,1)}, u32[]{:S(2)}, u32[]{:S(2)}) %collective-permute-start.18) | collective-permute-done | bytes 262176 | tf_op jit(solution)/shard_map/ppermute | solution.py:419
  119.1 41.9 %shard_map.60 = (f32[4,1024,1024]{2,1,0:T(8,128)}, bf16[1024,1024]{1,0:T(8,128)(2,1)}, f32[1,128]{1,0:T(1,128)}) custom-call(s32[1]{0:T(128)} %bitcast.me_ref, f32[1]{0:T(128)} %bitcast.3.scale_ref, bf16[8,2,128,1024]{3,2,1,0:T(8,128)(2,1)} %bitcast.10, f32[4,1024,1024]{2,1,0:T(8,128)} %bitcast.17, bf16[128,1024]{1,0:T(8,128)(2,1)} %copy-done.4, ...), custom_call_target="tpu_custom_call" | custom-call | flops 34359738368 | bytes 20971520 | tf_op jit(solution)/shard_map/pallas_call | solution.py:275
  161.0 4.8 %all-to-all-start = ((bf16[8,128,1024]{2,1,0:T(8,128)(2,1)}), bf16[8,128,1024]{2,1,0:T(8,128)(2,1)S(1)}, u32[]{:S(2)}, u32[]{:S(2)}) async-start(bf16[8,128,1024]{2,1,0:T(8,128)(2,1)} %bitcast.15), calls=%async_computation | async-start | bytes 4194304 | tf_op jit(solution)/shard_map/all_to_all | solution.py:434
  165.9 41.9 %shard_map.61 = (f32[4,1024,1024]{2,1,0:T(8,128)}, bf16[128,1024]{1,0:T(8,128)(2,1)}, bf16[128,1024]{1,0:T(8,128)(2,1)}, bf16[128,1024]{1,0:T(8,128)(2,1)}, bf16...) custom-call(s32[1]{0:T(128)} %bitcast.me_ref, ...), custom_call_target="tpu_custom_call", output_to_operand_aliasing={{0}: (11, {})} | custom-call | flops 34359738368 | bytes 20971520 | tf_op jit(solution)/shard_map/pallas_call | solution.py:275
  217.9 3.3 %collective-permute-start.28 = (f32[1,128]{1,0:T(1,128)S(1)}, f32[1,128]{1,0:T(1,128)S(1)}, u32[]{:S(2)}, u32[]{:S(2)}) collective-permute-start(f32[1,128]{1,0:T(1,128)S(1)} %add_add_fusion.1), channel_id=1, source_target_pairs={{0,8},{4,12},{8,16},{12,20},{16,24},{20,28},{24,0},{28,4},{1,9},{5... | collective-permute-start | bytes 1544 | tf_op jit(solution)/shard_map/ppermute | solution.py:425
  221.2 11.0 %collective-permute-done.27 = f32[1,128]{1,0:T(1,128)S(1)} collective-permute-done((f32[1,128]{1,0:T(1,128)S(1)}, f32[1,128]{1,0:T(1,128)S(1)}, u32[]{:S(2)}, u32[]{:S(2)}) %collective-permute-start.27) | collective-permute-done | bytes 544 | tf_op jit(solution)/shard_map/ppermute | solution.py:425
  232.2 4.8 %collective-permute-start.31 = (f32[1,128]{1,0:T(1,128)S(1)}, f32[1,128]{1,0:T(1,128)S(1)}, u32[]{:S(2)}, u32[]{:S(2)}) collective-permute-start(f32[1,128]{1,0:T(1,128)S(1)} %add_add_fusion.1), channel_id=1, source_target_pairs={{0,20},{4,24},{8,28},{12,0},{16,4},{20,8},{24,12},{28,16},{1,21},{... | collective-permute-start | bytes 1544 | tf_op jit(solution)/shard_map/ppermute | solution.py:425
  250.1 5.0 %collective-permute-done.37.rest_3_ = bf16[128,1024]{1,0:T(8,128)(2,1)S(1)} collective-permute-done((bf16[128,1024]{1,0:T(8,128)(2,1)}, bf16[128,1024]{1,0:T(8,128)(2,1)S(1)}, u32[]{:S(2)}, u32[]{:S(2)}) %collective-permute-start.37) | collective-permute-done | bytes 262176 | tf_op jit(solution)/shard_map/ppermute | solution.py:419
  255.1 3.4 %collective-permute-done.38.rest_4_ = bf16[128,1024]{1,0:T(8,128)(2,1)S(1)} collective-permute-done((bf16[128,1024]{1,0:T(8,128)(2,1)}, bf16[128,1024]{1,0:T(8,128)(2,1)S(1)}, u32[]{:S(2)}, u32[]{:S(2)}) %collective-permute-start.38) | collective-permute-done | bytes 262176 | tf_op jit(solution)/shard_map/ppermute | solution.py:419
  258.5 2.4 collective-permute-done.39.rest_5_
  (91 shorter events, 48.0 us)
Async XLA Ops:
  7.9 66.8 %collective-permute-start.10 = (bf16[128,1024]{1,0:T(8,128)(2,1)S(1)}, bf16[128,1024]{1,0:T(8,128)(2,1)S(1)}, u32[]{:S(2)}, u32[]{:S(2)}) collective-permute-start(bf16[128,1024]{1,0:T(8,128)(2,1)S(1)} %get-tuple-element.34), channel_id=1, source_target_pairs={{0,24},{4,28},{8,16},{12,20},{16,8},{20,12},{24,0},{28,4},{1,25},{... | collective-permute-start | bytes 786440 | tf_op jit(solution)/shard_map/ppermute | solution.py:419
  9.5 65.3 %collective-permute-start.11 = (bf16[128,1024]{1,0:T(8,128)(2,1)S(1)}, bf16[128,1024]{1,0:T(8,128)(2,1)S(1)}, u32[]{:S(2)}, u32[]{:S(2)}) collective-permute-start(bf16[128,1024]{1,0:T(8,128)(2,1)S(1)} %get-tuple-element.35), channel_id=1, source_target_pairs={{0,28},{4,24},{8,20},{12,16},{16,12},{20,8},{24,4},{28,0},{1,29},{... | collective-permute-start | bytes 786440 | tf_op jit(solution)/shard_map/ppermute | solution.py:419
  9.9 69.3 %collective-permute-start.12 = (bf16[128,1024]{1,0:T(8,128)(2,1)S(1)}, bf16[128,1024]{1,0:T(8,128)(2,1)S(1)}, u32[]{:S(2)}, u32[]{:S(2)}) collective-permute-start(bf16[128,1024]{1,0:T(8,128)(2,1)S(1)} %get-tuple-element.36), channel_id=1, source_target_pairs={{0,8},{4,12},{8,0},{12,4},{16,24},{20,28},{24,16},{28,20},{1,9},{5... | collective-permute-start | bytes 786440 | tf_op jit(solution)/shard_map/ppermute | solution.py:419
  12.1 67.1 %collective-permute-start.13 = (bf16[128,1024]{1,0:T(8,128)(2,1)S(1)}, bf16[128,1024]{1,0:T(8,128)(2,1)S(1)}, u32[]{:S(2)}, u32[]{:S(2)}) collective-permute-start(bf16[128,1024]{1,0:T(8,128)(2,1)S(1)} %get-tuple-element.37), channel_id=1, source_target_pairs={{0,12},{4,8},{8,4},{12,0},{16,28},{20,24},{24,20},{28,16},{1,13},{... | collective-permute-start | bytes 786440 | tf_op jit(solution)/shard_map/ppermute | solution.py:419
  13.1 20.9 %collective-permute-start.3 = (f32[1,128]{1,0:T(1,128)S(1)}, f32[1,128]{1,0:T(1,128)S(1)}, u32[]{:S(2)}, u32[]{:S(2)}) collective-permute-start(f32[1,128]{1,0:T(1,128)S(1)} %add_add_fusion.3), channel_id=1, source_target_pairs={{0,4},{4,8},{8,12},{12,16},{16,20},{20,24},{24,28},{28,0},{1,5},{5... | collective-permute-start | bytes 1544 | tf_op jit(solution)/shard_map/ppermute | solution.py:425
  74.7 18.2 %collective-permute-start.15 = (bf16[128,1024]{1,0:T(8,128)(2,1)S(1)}, bf16[128,1024]{1,0:T(8,128)(2,1)}, u32[]{:S(2)}, u32[]{:S(2)}) collective-permute-start(bf16[128,1024]{1,0:T(8,128)(2,1)S(1)} %get-tuple-element.39), channel_id=1, source_target_pairs={{0,20},{4,16},{8,28},{12,24},{16,4},{20,0},{24,12},{28,8},{1,21},{... | collective-permute-start | bytes 786440 | tf_op jit(solution)/shard_map/ppermute | solution.py:419
  74.8 21.3 %collective-permute-start.16 = (bf16[128,1024]{1,0:T(8,128)(2,1)S(1)}, bf16[128,1024]{1,0:T(8,128)(2,1)}, u32[]{:S(2)}, u32[]{:S(2)}) collective-permute-start(bf16[128,1024]{1,0:T(8,128)(2,1)S(1)} %get-tuple-element.40), channel_id=1, source_target_pairs={{0,4},{4,0},{8,12},{12,8},{16,20},{20,16},{24,28},{28,24},{1,5},{5... | collective-permute-start | bytes 786440 | tf_op jit(solution)/shard_map/ppermute | solution.py:419
  79.2 20.2 %collective-permute-start.17 = (bf16[128,1024]{1,0:T(8,128)(2,1)S(1)}, bf16[128,1024]{1,0:T(8,128)(2,1)}, u32[]{:S(2)}, u32[]{:S(2)}) collective-permute-start(bf16[128,1024]{1,0:T(8,128)(2,1)S(1)} %get-tuple-element.42), channel_id=1, source_target_pairs={{0,24},{4,28},{8,16},{12,20},{16,8},{20,12},{24,0},{28,4},{1,25},{... | collective-permute-start | bytes 786440 | tf_op jit(solution)/shard_map/ppermute | solution.py:419
  79.2 39.9 %collective-permute-start.18 = (bf16[128,1024]{1,0:T(8,128)(2,1)S(1)}, bf16[128,1024]{1,0:T(8,128)(2,1)}, u32[]{:S(2)}, u32[]{:S(2)}) collective-permute-start(bf16[128,1024]{1,0:T(8,128)(2,1)S(1)} %get-tuple-element.43), channel_id=1, source_target_pairs={{0,28},{4,24},{8,20},{12,16},{16,12},{20,8},{24,4},{28,0},{1,29},{... | collective-permute-start | bytes 786440 | tf_op jit(solution)/shard_map/ppermute | solution.py:419
  88.1 77.7 %collective-permute-start.19 = (bf16[128,1024]{1,0:T(8,128)(2,1)S(1)}, bf16[128,1024]{1,0:T(8,128)(2,1)}, u32[]{:S(2)}, u32[]{:S(2)}) collective-permute-start(bf16[128,1024]{1,0:T(8,128)(2,1)S(1)} %get-tuple-element.44), channel_id=1, source_target_pairs={{0,8},{4,12},{8,0},{12,4},{16,24},{20,28},{24,16},{28,20},{1,9},{5... | collective-permute-start | bytes 786440 | tf_op jit(solution)/shard_map/ppermute | solution.py:419
  92.9 72.9 %collective-permute-start.20 = (bf16[128,1024]{1,0:T(8,128)(2,1)S(1)}, bf16[128,1024]{1,0:T(8,128)(2,1)}, u32[]{:S(2)}, u32[]{:S(2)}) collective-permute-start(bf16[128,1024]{1,0:T(8,128)(2,1)S(1)} %get-tuple-element.45), channel_id=1, source_target_pairs={{0,12},{4,8},{8,4},{12,0},{16,28},{20,24},{24,20},{28,16},{1,13},{... | collective-permute-start | bytes 786440 | tf_op jit(solution)/shard_map/ppermute | solution.py:419
  96.1 69.7 %collective-permute-start.21 = (bf16[128,1024]{1,0:T(8,128)(2,1)S(1)}, bf16[128,1024]{1,0:T(8,128)(2,1)}, u32[]{:S(2)}, u32[]{:S(2)}) collective-permute-start(bf16[128,1024]{1,0:T(8,128)(2,1)S(1)} %get-tuple-element.46), channel_id=1, source_target_pairs={{0,16},{4,20},{8,24},{12,28},{16,0},{20,4},{24,8},{28,12},{1,17},{... | collective-permute-start | bytes 786440 | tf_op jit(solution)/shard_map/ppermute | solution.py:419
  99.4 66.4 %collective-permute-start.22 = (bf16[128,1024]{1,0:T(8,128)(2,1)S(1)}, bf16[128,1024]{1,0:T(8,128)(2,1)}, u32[]{:S(2)}, u32[]{:S(2)}) collective-permute-start(bf16[128,1024]{1,0:T(8,128)(2,1)S(1)} %get-tuple-element.47), channel_id=1, source_target_pairs={{0,20},{4,16},{8,28},{12,24},{16,4},{20,0},{24,12},{28,8},{1,21},{... | collective-permute-start | bytes 786440 | tf_op jit(solution)/shard_map/ppermute | solution.py:419
  119.1 46.7 %collective-permute-start.23 = (bf16[128,1024]{1,0:T(8,128)(2,1)S(1)}, bf16[128,1024]{1,0:T(8,128)(2,1)}, u32[]{:S(2)}, u32[]{:S(2)}) collective-permute-start(bf16[128,1024]{1,0:T(8,128)(2,1)S(1)} %get-tuple-element.48), channel_id=1, source_target_pairs={{0,4},{4,0},{8,12},{12,8},{16,20},{20,16},{24,28},{28,24},{1,5},{5... | collective-permute-start | bytes 786440 | tf_op jit(solution)/shard_map/ppermute | solution.py:419
  161.0 86.7 %all-to-all-start = ((bf16[8,128,1024]{2,1,0:T(8,128)(2,1)}), bf16[8,128,1024]{2,1,0:T(8,128)(2,1)S(1)}, u32[]{:S(2)}, u32[]{:S(2)}) async-start(bf16[8,128,1024]{2,1,0:T(8,128)(2,1)} %bitcast.15), calls=%async_computation | async-start | bytes 4194304 | tf_op jit(solution)/shard_map/all_to_all | solution.py:434
  207.8 35.7 %collective-permute-start.35 = (bf16[128,1024]{1,0:T(8,128)(2,1)}, bf16[128,1024]{1,0:T(8,128)(2,1)S(1)}, u32[]{:S(2)}, u32[]{:S(2)}) collective-permute-start(bf16[128,1024]{1,0:T(8,128)(2,1)} %get-tuple-element.53), channel_id=1, source_target_pairs={{0,24},{4,28},{8,16},{12,20},{16,8},{20,12},{24,0},{28,4},{1,25},{... | collective-permute-start | bytes 786440 | tf_op jit(solution)/shard_map/ppermute | solution.py:419
  209.3 34.7 %collective-permute-start.36 = (bf16[128,1024]{1,0:T(8,128)(2,1)}, bf16[128,1024]{1,0:T(8,128)(2,1)S(1)}, u32[]{:S(2)}, u32[]{:S(2)}) collective-permute-start(bf16[128,1024]{1,0:T(8,128)(2,1)} %get-tuple-element.54), channel_id=1, source_target_pairs={{0,28},{4,24},{8,20},{12,16},{16,12},{20,8},{24,4},{28,0},{1,29},{... | collective-permute-start | bytes 786440 | tf_op jit(solution)/shard_map/ppermute | solution.py:419
  215.5 16.7 %collective-permute-start.27 = (f32[1,128]{1,0:T(1,128)S(1)}, f32[1,128]{1,0:T(1,128)S(1)}, u32[]{:S(2)}, u32[]{:S(2)}) collective-permute-start(f32[1,128]{1,0:T(1,128)S(1)} %add_add_fusion.1), channel_id=1, source_target_pairs={{0,4},{4,8},{8,12},{12,16},{16,20},{20,24},{24,28},{28,0},{1,5},{5... | collective-permute-start | bytes 1544 | tf_op jit(solution)/shard_map/ppermute | solution.py:425
  221.1 15.9 %collective-permute-start.29 = (f32[1,128]{1,0:T(1,128)S(1)}, f32[1,128]{1,0:T(1,128)S(1)}, u32[]{:S(2)}, u32[]{:S(2)}) collective-permute-start(f32[1,128]{1,0:T(1,128)S(1)} %add_add_fusion.1), channel_id=1, source_target_pairs={{0,12},{4,16},{8,20},{12,24},{16,28},{20,0},{24,4},{28,8},{1,13},{... | collective-permute-start | bytes 1544 | tf_op jit(solution)/shard_map/ppermute | solution.py:425
  238.3 16.7 %collective-permute-start.37 = (bf16[128,1024]{1,0:T(8,128)(2,1)}, bf16[128,1024]{1,0:T(8,128)(2,1)S(1)}, u32[]{:S(2)}, u32[]{:S(2)}) collective-permute-start(bf16[128,1024]{1,0:T(8,128)(2,1)} %get-tuple-element.55), channel_id=1, source_target_pairs={{0,8},{4,12},{8,0},{12,4},{16,24},{20,28},{24,16},{28,20},{1,9},{5... | collective-permute-start | bytes 786440 | tf_op jit(solution)/shard_map/ppermute | solution.py:419
  240.6 17.9 %collective-permute-start.38 = (bf16[128,1024]{1,0:T(8,128)(2,1)}, bf16[128,1024]{1,0:T(8,128)(2,1)S(1)}, u32[]{:S(2)}, u32[]{:S(2)}) collective-permute-start(bf16[128,1024]{1,0:T(8,128)(2,1)} %get-tuple-element.56), channel_id=1, source_target_pairs={{0,12},{4,8},{8,4},{12,0},{16,28},{20,24},{24,20},{28,16},{1,13},{... | collective-permute-start | bytes 786440 | tf_op jit(solution)/shard_map/ppermute | solution.py:419
  241.6 19.3 %collective-permute-start.39 = (bf16[128,1024]{1,0:T(8,128)(2,1)}, bf16[128,1024]{1,0:T(8,128)(2,1)}, u32[]{:S(2)}, u32[]{:S(2)}) collective-permute-start(bf16[128,1024]{1,0:T(8,128)(2,1)} %get-tuple-element.57), channel_id=1, source_target_pairs={{0,16},{4,20},{8,24},{12,28},{16,0},{20,4},{24,8},{28,12},{1,17},{... | collective-permute-start | bytes 786440 | tf_op jit(solution)/shard_map/ppermute | solution.py:419
  243.5 17.4 %collective-permute-start.40 = (bf16[128,1024]{1,0:T(8,128)(2,1)}, bf16[128,1024]{1,0:T(8,128)(2,1)}, u32[]{:S(2)}, u32[]{:S(2)}) collective-permute-start(bf16[128,1024]{1,0:T(8,128)(2,1)} %get-tuple-element.58), channel_id=1, source_target_pairs={{0,4},{4,0},{8,12},{12,8},{16,20},{20,16},{24,28},{28,24},{1,5},{5... | collective-permute-start | bytes 786440 | tf_op jit(solution)/shard_map/ppermute | solution.py:419
  244.0 20.8 %collective-permute-start.34 = (bf16[128,1024]{1,0:T(8,128)(2,1)}, bf16[128,1024]{1,0:T(8,128)(2,1)}, u32[]{:S(2)}, u32[]{:S(2)}) collective-permute-start(bf16[128,1024]{1,0:T(8,128)(2,1)} %get-tuple-element.51), channel_id=1, source_target_pairs={{0,20},{4,16},{8,28},{12,24},{16,4},{20,0},{24,12},{28,8},{1,21},{... | collective-permute-start | bytes 786440 | tf_op jit(solution)/shard_map/ppermute | solution.py:419
  (26 other events, 330.3 us)

commit v4 on v3

--- a/solution.py
+++ b/solution.py
@@ -237,20 +237,26 @@
     lax.fori_loop(0, 2, root_step, 0)
     for start, stop in panels(width):
         square[:, start:stop] = dot_f32(left_root[...], grads[0, :, start:stop]).astype(jnp.bfloat16)
-    total = jnp.zeros((8, PANEL), jnp.float32)
-    for start, stop in panels(width):
-        value = dot_f32(square[...], root[:, start:stop])
-        fourth[:, start:stop] = value.astype(jnp.bfloat16)
-        total = total + lane_sums(value * value)
+    sends = []
     if whole:
-        sends = [pltpu.make_async_copy(fourth, prod_outs[0], sem_p.at[0])]
+        total = jnp.zeros((8, width), jnp.float32)
+        for n, (start, stop) in enumerate(panels(width)):
+            value = dot_f32(square[start:stop, :], root[...])
+            fourth[start:stop, :] = value.astype(jnp.bfloat16)
+            total = total + lane_sums(value * value)
+            send = pltpu.make_async_copy(fourth.at[start:stop, :], prod_outs[0].at[start:stop, :], sem_p.at[n])
+            send.start()
+            sends.append(send)
     else:
-        sends = [
-            pltpu.make_async_copy(fourth.at[rows_of(partner), :], prod_outs[n], sem_p.at[n])
-            for n, partner in enumerate((0, *partners))
-        ]
-    for send in sends:
-        send.start()
+        total = jnp.zeros((8, PANEL), jnp.float32)
+        for start, stop in panels(width):
+            value = dot_f32(square[...], root[:, start:stop])
+            fourth[:, start:stop] = value.astype(jnp.bfloat16)
+            total = total + lane_sums(value * value)
+        for n, partner in enumerate((0, *partners)):
+            send = pltpu.make_async_copy(fourth.at[rows_of(partner), :], prod_outs[n], sem_p.at[n])
+            send.start()
+            sends.append(send)
     squares_out[...] = jnp.broadcast_to(jnp.sum(total, keepdims=True), squares_out.shape)
     stat_done.wait()
     for send in sends:
@@ -290,7 +296,7 @@
             pltpu.SemaphoreType.DMA((len(partners) + 1,)),
             pltpu.SemaphoreType.DMA((2,)),
             pltpu.SemaphoreType.DMA,
-            pltpu.SemaphoreType.DMA((len(partners) + 1,)),
+            pltpu.SemaphoreType.DMA((max(len(partners) + 1, width // PANEL),)),
         ],
         input_output_aliases=aliases,
         compiler_params=pltpu.CompilerParams(vmem_limit_bytes=58 * 1024 * 1024),

time: 272 us -> 272 us (level)
  no operation moved by 1% of the time
where the time goes in v4:
time: 272 us; the launch traced here: 266 us
  waiting for transfers between devices  99.4 us (37%)
  Pallas kernels  91.8 us (34%)
  starting transfers between devices  61.2 us (22%)
  other arithmetic  8.76 us (3%)
  local copies, waits for them, and re-layouts  2.8 us (1%)
    pallas_call x2, Pallas kernels, block_call(): pl.pallas_call(functools.partial(block_kernel, block, partners, whole), o...  83.3 us
    ppermute x20, waiting for transfers between devices, sum_over(): lax.ppermute(value, axis, [(i, (i + shift) % size) for i in range(size)])  60.1 us
    ppermute x21, waiting for transfers between devices, swap(): return lax.ppermute(piece, 'dp', [(i, i ^ partner) for i in range(size)])  39.3 us
    ppermute x20, starting transfers between devices, sum_over(): lax.ppermute(value, axis, [(i, (i + shift) % size) for i in range(size)])  32.6 us
    ppermute x21, starting transfers between devices, swap(): return lax.ppermute(piece, 'dp', [(i, i ^ partner) for i in range(size)])  23.8 us
    reduce_sum x1, other arithmetic, on_device(): graft_squares = jnp.sum(graft_step * graft_step)  7.38 us
    pallas_call x3, Pallas kernels, scale_call(): pl.pallas_call(functools.partial(scale_kernel, chunk, targets), out_shape...  6.43 us
  transfers between devices with their start and end apart: 42, of which 21 were waited for; matrix products, arithmetic and copies ran while one was open for 4% of the time, Pallas kernels for 33%

profile of v4, /device:TPU:12, one launch (start us, length us, event | category | flops | bytes accessed | tf_op | source)
XLA Modules:
  0.0 266.2 jit_solution(6439855495375898388)
XLA Ops:
  13.1 2.7 %collective-permute-start.3 = (f32[1,128]{1,0:T(1,128)S(1)}, f32[1,128]{1,0:T(1,128)S(1)}, u32[]{:S(2)}, u32[]{:S(2)}) collective-permute-start(f32[1,128]{1,0:T(1,128)S(1)} %add_add_fusion.3), channel_id=1, source_target_pairs={{0,4},{4,8},{8,12},{12,16},{16,20},{20,24},{24,28},{28,0},{1,5},{5... | collective-permute-start | bytes 1544 | tf_op jit(solution)/shard_map/ppermute | solution.py:431
  15.8 18.2 %collective-permute-done.3 = f32[1,128]{1,0:T(1,128)S(1)} collective-permute-done((f32[1,128]{1,0:T(1,128)S(1)}, f32[1,128]{1,0:T(1,128)S(1)}, u32[]{:S(2)}, u32[]{:S(2)}) %collective-permute-start.3) | collective-permute-done | bytes 544 | tf_op jit(solution)/shard_map/ppermute | solution.py:431
  34.7 3.8 %collective-permute-done.4 = f32[1,128]{1,0:T(1,128)S(1)} collective-permute-done((f32[1,128]{1,0:T(1,128)S(1)}, f32[1,128]{1,0:T(1,128)S(1)}, u32[]{:S(2)}, u32[]{:S(2)}) %collective-permute-start.4) | collective-permute-done | bytes 544 | tf_op jit(solution)/shard_map/ppermute | solution.py:431
  38.5 3.3 %collective-permute-start.5 = (f32[1,128]{1,0:T(1,128)S(1)}, f32[1,128]{1,0:T(1,128)S(1)}, u32[]{:S(2)}, u32[]{:S(2)}) collective-permute-start(f32[1,128]{1,0:T(1,128)S(1)} %add_add_fusion.3), channel_id=1, source_target_pairs={{0,12},{4,16},{8,20},{12,24},{16,28},{20,0},{24,4},{28,8},{1,13},{... | collective-permute-start | bytes 1544 | tf_op jit(solution)/shard_map/ppermute | solution.py:431
  41.8 3.3 %collective-permute-done.5 = f32[1,128]{1,0:T(1,128)S(1)} collective-permute-done((f32[1,128]{1,0:T(1,128)S(1)}, f32[1,128]{1,0:T(1,128)S(1)}, u32[]{:S(2)}, u32[]{:S(2)}) %collective-permute-start.5) | collective-permute-done | bytes 544 | tf_op jit(solution)/shard_map/ppermute | solution.py:431
  46.2 3.4 %collective-permute-done.6 = f32[1,128]{1,0:T(1,128)S(1)} collective-permute-done((f32[1,128]{1,0:T(1,128)S(1)}, f32[1,128]{1,0:T(1,128)S(1)}, u32[]{:S(2)}, u32[]{:S(2)}) %collective-permute-start.6) | collective-permute-done | bytes 544 | tf_op jit(solution)/shard_map/ppermute | solution.py:431
  49.5 3.8 %collective-permute-start.7 = (f32[1,128]{1,0:T(1,128)S(1)}, f32[1,128]{1,0:T(1,128)S(1)}, u32[]{:S(2)}, u32[]{:S(2)}) collective-permute-start(f32[1,128]{1,0:T(1,128)S(1)} %add_add_fusion.3), channel_id=1, source_target_pairs={{0,20},{4,24},{8,28},{12,0},{16,4},{20,8},{24,12},{28,16},{1,21},{... | collective-permute-start | bytes 1544 | tf_op jit(solution)/shard_map/ppermute | solution.py:431
  54.9 3.5 %collective-permute-start.8 = (f32[1,128]{1,0:T(1,128)S(1)}, f32[1,128]{1,0:T(1,128)S(1)}, u32[]{:S(2)}, u32[]{:S(2)}) collective-permute-start(f32[1,128]{1,0:T(1,128)S(1)} %add_add_fusion.3), channel_id=1, source_target_pairs={{0,24},{4,28},{8,0},{12,4},{16,8},{20,12},{24,16},{28,20},{1,25},{... | collective-permute-start | bytes 1544 | tf_op jit(solution)/shard_map/ppermute | solution.py:431
  60.4 14.1 %collective-permute-done.9 = f32[1,128]{1,0:T(1,128)S(1)} collective-permute-done((f32[1,128]{1,0:T(1,128)S(1)}, f32[1,128]{1,0:T(1,128)S(1)}, u32[]{:S(2)}, u32[]{:S(2)}) %collective-permute-start.9) | collective-permute-done | bytes 544 | tf_op jit(solution)/shard_map/ppermute | solution.py:431
  74.8 4.4 %collective-permute-start.16 = (bf16[128,1024]{1,0:T(8,128)(2,1)S(1)}, bf16[128,1024]{1,0:T(8,128)(2,1)}, u32[]{:S(2)}, u32[]{:S(2)}) collective-permute-start(bf16[128,1024]{1,0:T(8,128)(2,1)S(1)} %get-tuple-element.40), channel_id=1, source_target_pairs={{0,4},{4,0},{8,12},{12,8},{16,20},{20,16},{24,28},{28,24},{1,5},{5... | collective-permute-start | bytes 786440 | tf_op jit(solution)/shard_map/ppermute | solution.py:425
  80.7 7.4 %multiply_reduce_fusion = (f32[]{:T(128)}, f32[4,4,128,1024]{3,2,1,0:T(8,128)}) fusion(bf16[4,4,128,1024]{3,2,1,0:T(8,128)(2,1)S(1)} %copy-done.1, f32[]{:T(128)} %bitcast.2, f32[4,4,128,1024]{3,2,1,0:T(8,128)} %param.5), kind=kLoop, calls=%fused_computation | loop fusion | flops 14680063 | bytes 20971528 | tf_op jit(solution)/shard_map/reduce_sum | solution.py:469
  88.8 4.1 %collective-permute-done.15.rest_5_ = bf16[128,1024]{1,0:T(8,128)(2,1)} collective-permute-done((bf16[128,1024]{1,0:T(8,128)(2,1)S(1)}, bf16[128,1024]{1,0:T(8,128)(2,1)}, u32[]{:S(2)}, u32[]{:S(2)}) %collective-permute-start.15) | collective-permute-done | bytes 262176 | tf_op jit(solution)/shard_map/ppermute | solution.py:425
  92.9 3.2 %collective-permute-start.20 = (bf16[128,1024]{1,0:T(8,128)(2,1)S(1)}, bf16[128,1024]{1,0:T(8,128)(2,1)}, u32[]{:S(2)}, u32[]{:S(2)}) collective-permute-start(bf16[128,1024]{1,0:T(8,128)(2,1)S(1)} %get-tuple-element.45), channel_id=1, source_target_pairs={{0,12},{4,8},{8,4},{12,0},{16,28},{20,24},{24,20},{28,16},{1,13},{... | collective-permute-start | bytes 786440 | tf_op jit(solution)/shard_map/ppermute | solution.py:425
  96.1 3.2 %collective-permute-done.17.rest_0_ = bf16[128,1024]{1,0:T(8,128)(2,1)} collective-permute-done((bf16[128,1024]{1,0:T(8,128)(2,1)S(1)}, bf16[128,1024]{1,0:T(8,128)(2,1)}, u32[]{:S(2)}, u32[]{:S(2)}) %collective-permute-start.17) | collective-permute-done | bytes 262176 | tf_op jit(solution)/shard_map/ppermute | solution.py:425
  99.6 19.5 %collective-permute-done.18.rest_1_ = bf16[128,1024]{1,0:T(8,128)(2,1)} collective-permute-done((bf16[128,1024]{1,0:T(8,128)(2,1)S(1)}, bf16[128,1024]{1,0:T(8,128)(2,1)}, u32[]{:S(2)}, u32[]{:S(2)}) %collective-permute-start.18) | collective-permute-done | bytes 262176 | tf_op jit(solution)/shard_map/ppermute | solution.py:425
  119.1 41.4 %shard_map.60 = (f32[4,1024,1024]{2,1,0:T(8,128)}, bf16[1024,1024]{1,0:T(8,128)(2,1)}, f32[1,128]{1,0:T(1,128)}) custom-call(s32[1]{0:T(128)} %bitcast.me_ref, f32[1]{0:T(128)} %bitcast.3.scale_ref, bf16[8,2,128,1024]{3,2,1,0:T(8,128)(2,1)} %bitcast.10, f32[4,1024,1024]{2,1,0:T(8,128)} %bitcast.17, bf16[128,1024]{1,0:T(8,128)(2,1)} %copy-done.4, ...), custom_call_target="tpu_custom_call" | custom-call | flops 34359738368 | bytes 20971520 | tf_op jit(solution)/shard_map/pallas_call | solution.py:281
  160.5 4.8 %all-to-all-start = ((bf16[8,128,1024]{2,1,0:T(8,128)(2,1)}), bf16[8,128,1024]{2,1,0:T(8,128)(2,1)S(1)}, u32[]{:S(2)}, u32[]{:S(2)}) async-start(bf16[8,128,1024]{2,1,0:T(8,128)(2,1)} %bitcast.15), calls=%async_computation | async-start | bytes 4194304 | tf_op jit(solution)/shard_map/all_to_all | solution.py:440
  165.3 41.9 %shard_map.61 = (f32[4,1024,1024]{2,1,0:T(8,128)}, bf16[128,1024]{1,0:T(8,128)(2,1)}, bf16[128,1024]{1,0:T(8,128)(2,1)}, bf16[128,1024]{1,0:T(8,128)(2,1)}, bf16...) custom-call(s32[1]{0:T(128)} %bitcast.me_ref, ...), custom_call_target="tpu_custom_call", output_to_operand_aliasing={{0}: (11, {})} | custom-call | flops 34359738368 | bytes 20971520 | tf_op jit(solution)/shard_map/pallas_call | solution.py:281
  217.3 3.3 %collective-permute-start.28 = (f32[1,128]{1,0:T(1,128)S(1)}, f32[1,128]{1,0:T(1,128)S(1)}, u32[]{:S(2)}, u32[]{:S(2)}) collective-permute-start(f32[1,128]{1,0:T(1,128)S(1)} %add_add_fusion.1), channel_id=1, source_target_pairs={{0,8},{4,12},{8,16},{12,20},{16,24},{20,28},{24,0},{28,4},{1,9},{5... | collective-permute-start | bytes 1544 | tf_op jit(solution)/shard_map/ppermute | solution.py:431
  220.7 11.0 %collective-permute-done.27 = f32[1,128]{1,0:T(1,128)S(1)} collective-permute-done((f32[1,128]{1,0:T(1,128)S(1)}, f32[1,128]{1,0:T(1,128)S(1)}, u32[]{:S(2)}, u32[]{:S(2)}) %collective-permute-start.27) | collective-permute-done | bytes 544 | tf_op jit(solution)/shard_map/ppermute | solution.py:431
  231.7 4.8 %collective-permute-start.31 = (f32[1,128]{1,0:T(1,128)S(1)}, f32[1,128]{1,0:T(1,128)S(1)}, u32[]{:S(2)}, u32[]{:S(2)}) collective-permute-start(f32[1,128]{1,0:T(1,128)S(1)} %add_add_fusion.1), channel_id=1, source_target_pairs={{0,20},{4,24},{8,28},{12,0},{16,4},{20,8},{24,12},{28,16},{1,21},{... | collective-permute-start | bytes 1544 | tf_op jit(solution)/shard_map/ppermute | solution.py:431
  249.6 5.0 %collective-permute-done.37.rest_3_ = bf16[128,1024]{1,0:T(8,128)(2,1)S(1)} collective-permute-done((bf16[128,1024]{1,0:T(8,128)(2,1)}, bf16[128,1024]{1,0:T(8,128)(2,1)S(1)}, u32[]{:S(2)}, u32[]{:S(2)}) %collective-permute-start.37) | collective-permute-done | bytes 262176 | tf_op jit(solution)/shard_map/ppermute | solution.py:425
  254.6 3.4 %collective-permute-done.38.rest_4_ = bf16[128,1024]{1,0:T(8,128)(2,1)S(1)} collective-permute-done((bf16[128,1024]{1,0:T(8,128)(2,1)}, bf16[128,1024]{1,0:T(8,128)(2,1)S(1)}, u32[]{:S(2)}, u32[]{:S(2)}) %collective-permute-start.38) | collective-permute-done | bytes 262176 | tf_op jit(solution)/shard_map/ppermute | solution.py:425
  258.0 2.4 collective-permute-done.39.rest_5_
  (91 shorter events, 48.0 us)
Async XLA Ops:
  7.9 66.8 %collective-permute-start.10 = (bf16[128,1024]{1,0:T(8,128)(2,1)S(1)}, bf16[128,1024]{1,0:T(8,128)(2,1)S(1)}, u32[]{:S(2)}, u32[]{:S(2)}) collective-permute-start(bf16[128,1024]{1,0:T(8,128)(2,1)S(1)} %get-tuple-element.34), channel_id=1, source_target_pairs={{0,24},{4,28},{8,16},{12,20},{16,8},{20,12},{24,0},{28,4},{1,25},{... | collective-permute-start | bytes 786440 | tf_op jit(solution)/shard_map/ppermute | solution.py:425
  9.5 65.3 %collective-permute-start.11 = (bf16[128,1024]{1,0:T(8,128)(2,1)S(1)}, bf16[128,1024]{1,0:T(8,128)(2,1)S(1)}, u32[]{:S(2)}, u32[]{:S(2)}) collective-permute-start(bf16[128,1024]{1,0:T(8,128)(2,1)S(1)} %get-tuple-element.35), channel_id=1, source_target_pairs={{0,28},{4,24},{8,20},{12,16},{16,12},{20,8},{24,4},{28,0},{1,29},{... | collective-permute-start | bytes 786440 | tf_op jit(solution)/shard_map/ppermute | solution.py:425
  9.9 69.3 %collective-permute-start.12 = (bf16[128,1024]{1,0:T(8,128)(2,1)S(1)}, bf16[128,1024]{1,0:T(8,128)(2,1)S(1)}, u32[]{:S(2)}, u32[]{:S(2)}) collective-permute-start(bf16[128,1024]{1,0:T(8,128)(2,1)S(1)} %get-tuple-element.36), channel_id=1, source_target_pairs={{0,8},{4,12},{8,0},{12,4},{16,24},{20,28},{24,16},{28,20},{1,9},{5... | collective-permute-start | bytes 786440 | tf_op jit(solution)/shard_map/ppermute | solution.py:425
  12.1 67.1 %collective-permute-start.13 = (bf16[128,1024]{1,0:T(8,128)(2,1)S(1)}, bf16[128,1024]{1,0:T(8,128)(2,1)S(1)}, u32[]{:S(2)}, u32[]{:S(2)}) collective-permute-start(bf16[128,1024]{1,0:T(8,128)(2,1)S(1)} %get-tuple-element.37), channel_id=1, source_target_pairs={{0,12},{4,8},{8,4},{12,0},{16,28},{20,24},{24,20},{28,16},{1,13},{... | collective-permute-start | bytes 786440 | tf_op jit(solution)/shard_map/ppermute | solution.py:425
  13.1 20.9 %collective-permute-start.3 = (f32[1,128]{1,0:T(1,128)S(1)}, f32[1,128]{1,0:T(1,128)S(1)}, u32[]{:S(2)}, u32[]{:S(2)}) collective-permute-start(f32[1,128]{1,0:T(1,128)S(1)} %add_add_fusion.3), channel_id=1, source_target_pairs={{0,4},{4,8},{8,12},{12,16},{16,20},{20,24},{24,28},{28,0},{1,5},{5... | collective-permute-start | bytes 1544 | tf_op jit(solution)/shard_map/ppermute | solution.py:431
  74.7 18.2 %collective-permute-start.15 = (bf16[128,1024]{1,0:T(8,128)(2,1)S(1)}, bf16[128,1024]{1,0:T(8,128)(2,1)}, u32[]{:S(2)}, u32[]{:S(2)}) collective-permute-start(bf16[128,1024]{1,0:T(8,128)(2,1)S(1)} %get-tuple-element.39), channel_id=1, source_target_pairs={{0,20},{4,16},{8,28},{12,24},{16,4},{20,0},{24,12},{28,8},{1,21},{... | collective-permute-start | bytes 786440 | tf_op jit(solution)/shard_map/ppermute | solution.py:425
  74.8 21.3 %collective-permute-start.16 = (bf16[128,1024]{1,0:T(8,128)(2,1)S(1)}, bf16[128,1024]{1,0:T(8,128)(2,1)}, u32[]{:S(2)}, u32[]{:S(2)}) collective-permute-start(bf16[128,1024]{1,0:T(8,128)(2,1)S(1)} %get-tuple-element.40), channel_id=1, source_target_pairs={{0,4},{4,0},{8,12},{12,8},{16,20},{20,16},{24,28},{28,24},{1,5},{5... | collective-permute-start | bytes 786440 | tf_op jit(solution)/shard_map/ppermute | solution.py:425
  79.2 20.2 %collective-permute-start.17 = (bf16[128,1024]{1,0:T(8,128)(2,1)S(1)}, bf16[128,1024]{1,0:T(8,128)(2,1)}, u32[]{:S(2)}, u32[]{:S(2)}) collective-permute-start(bf16[128,1024]{1,0:T(8,128)(2,1)S(1)} %get-tuple-element.42), channel_id=1, source_target_pairs={{0,24},{4,28},{8,16},{12,20},{16,8},{20,12},{24,0},{28,4},{1,25},{... | collective-permute-start | bytes 786440 | tf_op jit(solution)/shard_map/ppermute | solution.py:425
  79.2 39.9 %collective-permute-start.18 = (bf16[128,1024]{1,0:T(8,128)(2,1)S(1)}, bf16[128,1024]{1,0:T(8,128)(2,1)}, u32[]{:S(2)}, u32[]{:S(2)}) collective-permute-start(bf16[128,1024]{1,0:T(8,128)(2,1)S(1)} %get-tuple-element.43), channel_id=1, source_target_pairs={{0,28},{4,24},{8,20},{12,16},{16,12},{20,8},{24,4},{28,0},{1,29},{... | collective-permute-start | bytes 786440 | tf_op jit(solution)/shard_map/ppermute | solution.py:425
  88.1 77.2 %collective-permute-start.19 = (bf16[128,1024]{1,0:T(8,128)(2,1)S(1)}, bf16[128,1024]{1,0:T(8,128)(2,1)}, u32[]{:S(2)}, u32[]{:S(2)}) collective-permute-start(bf16[128,1024]{1,0:T(8,128)(2,1)S(1)} %get-tuple-element.44), channel_id=1, source_target_pairs={{0,8},{4,12},{8,0},{12,4},{16,24},{20,28},{24,16},{28,20},{1,9},{5... | collective-permute-start | bytes 786440 | tf_op jit(solution)/shard_map/ppermute | solution.py:425
  92.9 72.4 %collective-permute-start.20 = (bf16[128,1024]{1,0:T(8,128)(2,1)S(1)}, bf16[128,1024]{1,0:T(8,128)(2,1)}, u32[]{:S(2)}, u32[]{:S(2)}) collective-permute-start(bf16[128,1024]{1,0:T(8,128)(2,1)S(1)} %get-tuple-element.45), channel_id=1, source_target_pairs={{0,12},{4,8},{8,4},{12,0},{16,28},{20,24},{24,20},{28,16},{1,13},{... | collective-permute-start | bytes 786440 | tf_op jit(solution)/shard_map/ppermute | solution.py:425
  96.1 69.2 %collective-permute-start.21 = (bf16[128,1024]{1,0:T(8,128)(2,1)S(1)}, bf16[128,1024]{1,0:T(8,128)(2,1)}, u32[]{:S(2)}, u32[]{:S(2)}) collective-permute-start(bf16[128,1024]{1,0:T(8,128)(2,1)S(1)} %get-tuple-element.46), channel_id=1, source_target_pairs={{0,16},{4,20},{8,24},{12,28},{16,0},{20,4},{24,8},{28,12},{1,17},{... | collective-permute-start | bytes 786440 | tf_op jit(solution)/shard_map/ppermute | solution.py:425
  99.4 65.9 %collective-permute-start.22 = (bf16[128,1024]{1,0:T(8,128)(2,1)S(1)}, bf16[128,1024]{1,0:T(8,128)(2,1)}, u32[]{:S(2)}, u32[]{:S(2)}) collective-permute-start(bf16[128,1024]{1,0:T(8,128)(2,1)S(1)} %get-tuple-element.47), channel_id=1, source_target_pairs={{0,20},{4,16},{8,28},{12,24},{16,4},{20,0},{24,12},{28,8},{1,21},{... | collective-permute-start | bytes 786440 | tf_op jit(solution)/shard_map/ppermute | solution.py:425
  119.1 46.2 %collective-permute-start.23 = (bf16[128,1024]{1,0:T(8,128)(2,1)S(1)}, bf16[128,1024]{1,0:T(8,128)(2,1)}, u32[]{:S(2)}, u32[]{:S(2)}) collective-permute-start(bf16[128,1024]{1,0:T(8,128)(2,1)S(1)} %get-tuple-element.48), channel_id=1, source_target_pairs={{0,4},{4,0},{8,12},{12,8},{16,20},{20,16},{24,28},{28,24},{1,5},{5... | collective-permute-start | bytes 786440 | tf_op jit(solution)/shard_map/ppermute | solution.py:425
  160.5 86.7 %all-to-all-start = ((bf16[8,128,1024]{2,1,0:T(8,128)(2,1)}), bf16[8,128,1024]{2,1,0:T(8,128)(2,1)S(1)}, u32[]{:S(2)}, u32[]{:S(2)}) async-start(bf16[8,128,1024]{2,1,0:T(8,128)(2,1)} %bitcast.15), calls=%async_computation | async-start | bytes 4194304 | tf_op jit(solution)/shard_map/all_to_all | solution.py:440
  207.2 35.7 %collective-permute-start.35 = (bf16[128,1024]{1,0:T(8,128)(2,1)}, bf16[128,1024]{1,0:T(8,128)(2,1)S(1)}, u32[]{:S(2)}, u32[]{:S(2)}) collective-permute-start(bf16[128,1024]{1,0:T(8,128)(2,1)} %get-tuple-element.53), channel_id=1, source_target_pairs={{0,24},{4,28},{8,16},{12,20},{16,8},{20,12},{24,0},{28,4},{1,25},{... | collective-permute-start | bytes 786440 | tf_op jit(solution)/shard_map/ppermute | solution.py:425
  208.8 34.7 %collective-permute-start.36 = (bf16[128,1024]{1,0:T(8,128)(2,1)}, bf16[128,1024]{1,0:T(8,128)(2,1)S(1)}, u32[]{:S(2)}, u32[]{:S(2)}) collective-permute-start(bf16[128,1024]{1,0:T(8,128)(2,1)} %get-tuple-element.54), channel_id=1, source_target_pairs={{0,28},{4,24},{8,20},{12,16},{16,12},{20,8},{24,4},{28,0},{1,29},{... | collective-permute-start | bytes 786440 | tf_op jit(solution)/shard_map/ppermute | solution.py:425
  215.0 16.7 %collective-permute-start.27 = (f32[1,128]{1,0:T(1,128)S(1)}, f32[1,128]{1,0:T(1,128)S(1)}, u32[]{:S(2)}, u32[]{:S(2)}) collective-permute-start(f32[1,128]{1,0:T(1,128)S(1)} %add_add_fusion.1), channel_id=1, source_target_pairs={{0,4},{4,8},{8,12},{12,16},{16,20},{20,24},{24,28},{28,0},{1,5},{5... | collective-permute-start | bytes 1544 | tf_op jit(solution)/shard_map/ppermute | solution.py:431
  220.6 15.9 %collective-permute-start.29 = (f32[1,128]{1,0:T(1,128)S(1)}, f32[1,128]{1,0:T(1,128)S(1)}, u32[]{:S(2)}, u32[]{:S(2)}) collective-permute-start(f32[1,128]{1,0:T(1,128)S(1)} %add_add_fusion.1), channel_id=1, source_target_pairs={{0,12},{4,16},{8,20},{12,24},{16,28},{20,0},{24,4},{28,8},{1,13},{... | collective-permute-start | bytes 1544 | tf_op jit(solution)/shard_map/ppermute | solution.py:431
  237.8 16.7 %collective-permute-start.37 = (bf16[128,1024]{1,0:T(8,128)(2,1)}, bf16[128,1024]{1,0:T(8,128)(2,1)S(1)}, u32[]{:S(2)}, u32[]{:S(2)}) collective-permute-start(bf16[128,1024]{1,0:T(8,128)(2,1)} %get-tuple-element.55), channel_id=1, source_target_pairs={{0,8},{4,12},{8,0},{12,4},{16,24},{20,28},{24,16},{28,20},{1,9},{5... | collective-permute-start | bytes 786440 | tf_op jit(solution)/shard_map/ppermute | solution.py:425
  240.1 17.9 %collective-permute-start.38 = (bf16[128,1024]{1,0:T(8,128)(2,1)}, bf16[128,1024]{1,0:T(8,128)(2,1)S(1)}, u32[]{:S(2)}, u32[]{:S(2)}) collective-permute-start(bf16[128,1024]{1,0:T(8,128)(2,1)} %get-tuple-element.56), channel_id=1, source_target_pairs={{0,12},{4,8},{8,4},{12,0},{16,28},{20,24},{24,20},{28,16},{1,13},{... | collective-permute-start | bytes 786440 | tf_op jit(solution)/shard_map/ppermute | solution.py:425
  241.1 19.3 %collective-permute-start.39 = (bf16[128,1024]{1,0:T(8,128)(2,1)}, bf16[128,1024]{1,0:T(8,128)(2,1)}, u32[]{:S(2)}, u32[]{:S(2)}) collective-permute-start(bf16[128,1024]{1,0:T(8,128)(2,1)} %get-tuple-element.57), channel_id=1, source_target_pairs={{0,16},{4,20},{8,24},{12,28},{16,0},{20,4},{24,8},{28,12},{1,17},{... | collective-permute-start | bytes 786440 | tf_op jit(solution)/shard_map/ppermute | solution.py:425
  243.0 17.4 %collective-permute-start.40 = (bf16[128,1024]{1,0:T(8,128)(2,1)}, bf16[128,1024]{1,0:T(8,128)(2,1)}, u32[]{:S(2)}, u32[]{:S(2)}) collective-permute-start(bf16[128,1024]{1,0:T(8,128)(2,1)} %get-tuple-element.58), channel_id=1, source_target_pairs={{0,4},{4,0},{8,12},{12,8},{16,20},{20,16},{24,28},{28,24},{1,5},{5... | collective-permute-start | bytes 786440 | tf_op jit(solution)/shard_map/ppermute | solution.py:425
  243.5 20.8 %collective-permute-start.34 = (bf16[128,1024]{1,0:T(8,128)(2,1)}, bf16[128,1024]{1,0:T(8,128)(2,1)}, u32[]{:S(2)}, u32[]{:S(2)}) collective-permute-start(bf16[128,1024]{1,0:T(8,128)(2,1)} %get-tuple-element.51), channel_id=1, source_target_pairs={{0,20},{4,16},{8,28},{12,24},{16,4},{20,0},{24,12},{28,8},{1,21},{... | collective-permute-start | bytes 786440 | tf_op jit(solution)/shard_map/ppermute | solution.py:425
  (26 other events, 330.3 us)
